TPU v7x, 32 devices: a whole 2x2x4 slice. The times are simulated.
32 devices in a mesh: tx: 4 (over z), ty: 2 (over y), vel: 4 (over x, core).
Axes of the slice: x: 2, y: 2, z: 4, core: 2. Of those that a mesh axis runs over, the one named last changes fastest.
Arguments:
- initial: float32 [32, 16, 16, 3072], P('tx', 'ty', None, 'vel'), may hold values from -2 to 3.5
- velocity: float32 [3, 3072], P(None, 'vel'), may hold values from -3 to 3, as said below
- weights: float32 [3072], P('vel'), may hold values from 0.5 to 2
- wall: int32 [32, 16, 16], P('tx', 'ty'), may hold values 0 or 1
- wall_temp: float32 [32, 16, 16], P('tx', 'ty'), may hold values from -1 to 1
- mass_target: float32 [], replicated, may hold values from 0.5 to 1.5
Outputs:
- distribution: float32 [32, 16, 16, 3072], P('tx', 'ty', None, 'vel')
- macro_fields: float32 [5, 32, 16, 16], P(None, 'tx', 'ty')
Inputs may be any that keep to these rules, and one draw needn't show every extreme that they name: `velocity`: within each aligned block of 768 velocities the first quarter has positive x and y components, the second positive x and negative y, the third negative x and positive y, the fourth negative x and y; x and y components are 0.05 or more in magnitude.
All inputs are finite; a program needn't handle non-finite values. No bound on the sum of `wall` on one device may be relied on, other than what follows from the above.
Results may differ from a plain program's by a relative error of at most 0.0003.
Values sent between devices are 32-bit elements; how exact they have to be, the bound alone decides.
No kernel may reach another device: no remote copies, remote signals or barrier semaphores. Data moves between devices by JAX's collectives and lax.ppermute only.
A program may use at most 128 MiB of HBM per device.

v0:
```python
import jax
import jax.numpy as jnp
from jax import lax
from jax.sharding import PartitionSpec as P

ITERS = 3
MACRO_STEPS = 4
step_time = 0.1
collision = 1.0
macro_time = 0.1
viscosity = 1.0
conduction = 1.0
highest = lax.Precision.HIGHEST


def padded_2(cells, sides, width):
    for axis, dim in sides:
        count = lax.axis_size(axis)
        head = lax.slice_in_dim(cells, 0, width, axis=dim)
        tail = lax.slice_in_dim(cells, cells.shape[dim] - width, cells.shape[dim], axis=dim)
        cells = jnp.concatenate(
            [
                lax.ppermute(tail, axis, [(i, (i + 1) % count) for i in range(count)]),
                cells,
                lax.ppermute(head, axis, [((i + 1) % count, i) for i in range(count)]),
            ],
            axis=dim,
        )
    return cells


def basis(velocity):
    speed_sq = velocity[0] * velocity[0] + velocity[1] * velocity[1] + velocity[2] * velocity[2]
    return jnp.stack(
        [
            jnp.ones_like(speed_sq),
            2.0 * velocity[0],
            2.0 * velocity[1],
            2.0 * velocity[2],
            speed_sq - 1.5,
        ]
    )


def projector(velocity, weights, total_count):
    vel_x, vel_y, vel_z = (velocity[0], velocity[1], velocity[2])
    speed_sq = vel_x * vel_x + vel_y * vel_y + vel_z * vel_z
    moment_rows = jnp.stack(
        [
            jnp.ones_like(speed_sq),
            vel_x,
            vel_y,
            vel_z,
            2.0 / 3.0 * speed_sq - 1.0,
            2.0 * (vel_x * vel_x - speed_sq / 3.0),
            2.0 * (vel_y * vel_y - speed_sq / 3.0),
            2.0 * (vel_z * vel_z - speed_sq / 3.0),
            2.0 * vel_x * vel_y,
            2.0 * vel_x * vel_z,
            2.0 * vel_y * vel_z,
            vel_x * (speed_sq - 2.5),
            vel_y * (speed_sq - 2.5),
            vel_z * (speed_sq - 2.5),
        ]
    )
    return moment_rows * (weights / total_count)[None, :]


def differences(shifted):
    grads = [(shifted(direction, 1) - shifted(direction, -1)) * 0.5 for direction in (1, 2, 3)]
    middle = shifted(1, 0)
    laplace = (
        shifted(1, 1)
        + shifted(1, -1)
        - 2.0 * middle
        + (shifted(2, 1) + shifted(2, -1) - 2.0 * middle)
    )
    laplace = laplace + (shifted(3, 1) + shifted(3, -1) - 2.0 * middle)
    return (grads, laplace, middle)


def macro_sources(shifted):
    grads, laplace, middle = differences(shifted)
    grad_x, grad_y, grad_z = grads
    sig_x = grad_x[0] + grad_y[3] + grad_z[4]
    sig_y = grad_x[3] + grad_y[1] + grad_z[5]
    sig_z = grad_x[4] + grad_y[5] + grad_z[2]
    heat_flow = grad_x[6] + grad_y[7] + grad_z[8]
    return jnp.stack(
        [
            -0.5 * (sig_x + viscosity * laplace[9]),
            -0.5 * (sig_y + viscosity * laplace[10]),
            -0.5 * (sig_z + viscosity * laplace[11]),
            -(2.0 / 3.0) * (heat_flow + conduction * laplace[12]),
        ]
    )


def macro_step(shifted, sources):
    grads, laplace, middle = differences(shifted)
    grad_x, grad_y, grad_z = grads
    div_u = grad_x[1] + grad_y[2] + grad_z[3]
    change_rates = [-div_u]
    for component in range(3):
        along = grads[component]
        change_rates.append(
            -0.5 * (along[0] + along[4])
            + 0.5 * viscosity * laplace[1 + component]
            + sources[component]
        )
    change_rates.append(-(2.0 / 3.0) * div_u + 2.0 / 3.0 * conduction * laplace[4] + sources[3])
    return middle + macro_time * jnp.stack(change_rates)


def kinetic_update(corrected, equilibrium, before_x, after_x, before_y, after_y, velocity):
    plus_part = jnp.maximum(velocity, 0.0)
    minus_part = jnp.minimum(velocity, 0.0)
    before_z = jnp.roll(corrected, 1, 2)
    after_z = jnp.roll(corrected, -1, 2)
    transport = plus_part[0] * (corrected - before_x) + minus_part[0] * (after_x - corrected)
    transport = transport + (
        plus_part[1] * (corrected - before_y) + minus_part[1] * (after_y - corrected)
    )
    transport = transport + (
        plus_part[2] * (corrected - before_z) + minus_part[2] * (after_z - corrected)
    )
    return corrected - step_time * transport + step_time * collision * (equilibrium - corrected)


def padded_view(padded):

    def shifted(direction, offset):
        selector = [slice(None), slice(1, -1), slice(1, -1), slice(1, -1)]
        extent = padded.shape[direction]
        selector[direction] = slice(1 + offset, extent - 1 + offset)
        return padded[tuple(selector)]

    return shifted


def wrap_depth(padded):
    return jnp.concatenate([padded[..., -1:], padded, padded[..., :1]], axis=3)


def pad_sources(fields):
    padded = wrap_depth(padded_2(fields, (("tx", 1), ("ty", 2)), 1))
    return padded


def pad_state(macro_state):
    padded = wrap_depth(padded_2(macro_state, (("tx", 1), ("ty", 2)), 1))
    return padded


def total_mass(local_sum):
    summed = lax.psum(local_sum, ("tx", "ty"))
    return summed


def on_device(initial, velocity, weights, wall, wall_temp, mass_target):
    width_dev = weights.shape[0]
    total_velocities = float(width_dev * lax.axis_size("vel"))
    cell_count = float(
        wall.shape[0] * wall.shape[1] * wall.shape[2] * lax.axis_size("tx") * lax.axis_size("ty")
    )
    moment_rows = projector(velocity, weights, total_velocities)
    rows = basis(velocity)
    is_wall = (wall == 1)[..., None]
    wall_state = wall_temp[..., None] * rows[4]
    distribution = initial
    macro_state = None
    for iteration in range(ITERS):
        local_moments = jnp.einsum("kv,xyzv->kxyz", moment_rows, distribution, precision=highest)
        moments = lax.psum(local_moments, "vel")
        kinetic_state = moments[0:5]
        fields = jnp.concatenate([moments[5:14], moments[1:5]])
        mass_total = total_mass(jnp.sum(kinetic_state[0]))
        sources = macro_sources(padded_view(pad_sources(fields)))
        macro_state = kinetic_state
        for sweep in range(MACRO_STEPS):
            macro_state = macro_step(padded_view(pad_state(macro_state)), sources)
        density_mean = mass_total / cell_count
        macro_state = jnp.concatenate(
            [(macro_state[0] - density_mean + mass_target)[None], macro_state[1:]]
        )
        change = macro_state - kinetic_state
        corrected = distribution + jnp.einsum("kxyz,kv->xyzv", change, rows, precision=highest)
        equilibrium = jnp.einsum("kxyz,kv->xyzv", macro_state, rows, precision=highest)
        padded = padded_2(corrected, (("tx", 0), ("ty", 1)), 1)
        before_x = padded[:-2, 1:-1]
        after_x = padded[2:, 1:-1]
        before_y = padded[1:-1, :-2]
        after_y = padded[1:-1, 2:]
        updated = kinetic_update(
            corrected, equilibrium, before_x, after_x, before_y, after_y, velocity
        )
        distribution = jnp.where(is_wall, wall_state, updated)
    return (distribution, macro_state)


def solution(mesh):
    placed = (
        P("tx", "ty", None, "vel"),
        P(None, "vel"),
        P("vel"),
        P("tx", "ty", None),
        P("tx", "ty", None),
        P(),
    )
    return jax.shard_map(
        on_device,
        mesh=mesh,
        in_specs=placed,
        out_specs=(P("tx", "ty", None, "vel"), P(None, "tx", "ty", None)),
        check_vma=False,
    )
```

profile of v0, /device:TPU:0, one launch (start us, length us, event | category | flops | bytes accessed | tf_op | source)
XLA Modules:
  0.0 449.7 jit_solution(716490009049969232)
XLA Ops:
  4.4 12.9 %fusion.73 = f32[14,8,8,16]{3,0,2,1:T(8,128)S(1)} fusion(f32[8,8,16,768]{3,2,1,0:T(8,128)} %param.6, f32[14,768]{1,0:T(8,128)S(1)} %stack.29, f32[768]{0:T(1024)S(1)} %broadcast_multiply_fusion), kind=kOutput, calls=%fused_computation.583 | convolution fusion | flops 132131328 | bytes 3249152 | tf_op jit(solution)/shard_map/kv,xyzv->kxyz/dot_general | solution.py:173
  17.5 17.4 %psum.42 = f32[14,8,8,16]{3,2,1,0:T(8,128)S(1)} all-reduce(f32[14,8,8,16]{3,2,1,0:T(8,128)S(1)} %copy.9), channel_id=1, replica_groups=mesh['tx'=4,'ty'=2,'vel'=4] {'vel'}, use_global_device_ids=true, to_apply=%region_0.0 | all-reduce | flops 14336 | bytes 114688 | tf_op jit(solution)/shard_map/psum | solution.py:174
  36.5 2.2 collective-permute-start
  44.1 2.7 collective-permute-start.4
  51.1 2.2 collective-permute-done.7
  58.4 2.8 collective-permute-start.8
  70.0 2.8 collective-permute-start.12
  82.4 2.6 collective-permute-start.16
  89.4 21.9 %psum.43 = f32[]{:T(128)} all-reduce(f32[]{:T(128)} %slice_reduce_fusion.2), channel_id=1, replica_groups=mesh['tx'=4,'ty'=2,'vel'=4] {'tx','ty'}, use_global_device_ids=true, to_apply=%region_2.0 | all-reduce | flops 1 | bytes 8 | tf_op jit(solution)/shard_map/psum | solution.py:156
  114.7 2.8 convolution_add_fusion.2
  117.6 4.2 collective-permute-start.21
  122.0 5.3 %collective-permute-done.20 = f32[1,8,16,768]{3,2,1,0:T(8,128)S(1)} collective-permute-done((f32[1,8,16,768]{3,2,1,0:T(8,128)S(1)}, f32[1,8,16,768]{3,2,1,0:T(8,128)S(1)}, u32[]{:S(2)}, u32[]{:S(2)}) %collective-permute-start.20) | collective-permute-done | bytes 393248 | tf_op jit(solution)/shard_map/ppermute | solution.py:23
  127.3 2.8 collective-permute-done.21
  133.1 5.9 %collective-permute-done.22 = f32[10,1,16,768]{3,2,1,0:T(8,128)S(1)} collective-permute-done((f32[10,1,16,768]{3,2,1,0:T(8,128)S(1)}, f32[10,1,16,768]{3,2,1,0:T(8,128)S(1)}, u32[]{:S(2)}, u32[]{:S(2)}) %collective-permute-start.22) | collective-permute-done | bytes 491552 | tf_op jit(solution)/shard_map/ppermute | solution.py:23
  139.0 5.3 %collective-permute-done.23 = f32[10,1,16,768]{3,2,1,0:T(8,128)S(1)} collective-permute-done((f32[10,1,16,768]{3,2,1,0:T(8,128)S(1)}, f32[10,1,16,768]{3,2,1,0:T(8,128)S(1)}, u32[]{:S(2)}, u32[]{:S(2)}) %collective-permute-start.23) | collective-permute-done | bytes 491552 | tf_op jit(solution)/shard_map/ppermute | solution.py:25
  144.4 6.1 %multiply_select_fusion.2 = f32[8,8,16,768]{3,2,1,0:T(8,128)S(1)} fusion(f32[8,8,16,768]{3,2,1,0:T(8,128)S(1)} %convolution_add_fusion.2, f32[10,1,16,768]{3,2,1,0:T(8,128)S(1)} %collective-permute-done.23, f32[1,8,16,768]{3,2,1,0:T(8,128)S(1)} %collective-permute-done.21, f32[1,8,16,768]{3,2,1,0:T(8,128)S(1)} %collective-permute-done.20, ...), kind=kOutput, calls=%fused_computation.2 | convolution fusion | flops 73924608 | bytes 14414848 | tf_op jit(solution)/shard_map/kxyz,kv->xyzv/dot_general | solution.py:188
  150.5 11.2 %fusion.71 = f32[14,8,8,16]{3,0,2,1:T(8,128)S(1)} fusion(f32[8,8,16,768]{3,2,1,0:T(8,128)S(1)} %multiply_select_fusion.2, f32[14,768]{1,0:T(8,128)S(1)} %stack.29, f32[768]{0:T(1024)S(1)} %broadcast_multiply_fusion), kind=kOutput, calls=%fused_computation.581 | convolution fusion | flops 132131328 | bytes 3249152 | tf_op jit(solution)/shard_map/kv,xyzv->kxyz/dot_general | solution.py:173
  162.6 16.1 %psum.44 = f32[14,8,8,16]{3,2,1,0:T(8,128)} all-reduce(f32[14,8,8,16]{3,2,1,0:T(8,128)} %copy.12), channel_id=1, replica_groups=mesh['tx'=4,'ty'=2,'vel'=4] {'vel'}, use_global_device_ids=true, to_apply=%region_3.4 | all-reduce | flops 14336 | bytes 114688 | tf_op jit(solution)/shard_map/psum | solution.py:174
  180.5 2.8 collective-permute-start.24
  188.4 3.8 collective-permute-start.28
  196.5 2.2 collective-permute-done.31
  202.9 3.8 collective-permute-start.32
  216.0 2.8 collective-permute-start.36
  227.6 2.7 collective-permute-start.40
  236.3 22.7 %psum.45 = f32[]{:T(128)} all-reduce(f32[]{:T(128)} %slice_reduce_fusion.1), channel_id=1, replica_groups=mesh['tx'=4,'ty'=2,'vel'=4] {'tx','ty'}, use_global_device_ids=true, to_apply=%region_5.6 | all-reduce | flops 1 | bytes 8 | tf_op jit(solution)/shard_map/psum | solution.py:156
  264.9 2.8 convolution_add_fusion.1
  267.9 4.2 collective-permute-start.45
  272.1 5.5 %collective-permute-done.44 = f32[1,8,16,768]{3,2,1,0:T(8,128)S(1)} collective-permute-done((f32[1,8,16,768]{3,2,1,0:T(8,128)S(1)}, f32[1,8,16,768]{3,2,1,0:T(8,128)S(1)}, u32[]{:S(2)}, u32[]{:S(2)}) %collective-permute-start.44) | collective-permute-done | bytes 393248 | tf_op jit(solution)/shard_map/ppermute | solution.py:23
  277.5 2.8 collective-permute-done.45
  283.4 5.9 %collective-permute-done.46 = f32[10,1,16,768]{3,2,1,0:T(8,128)S(1)} collective-permute-done((f32[10,1,16,768]{3,2,1,0:T(8,128)S(1)}, f32[10,1,16,768]{3,2,1,0:T(8,128)S(1)}, u32[]{:S(2)}, u32[]{:S(2)}) %collective-permute-start.46) | collective-permute-done | bytes 491552 | tf_op jit(solution)/shard_map/ppermute | solution.py:23
  289.3 5.3 %collective-permute-done.47 = f32[10,1,16,768]{3,2,1,0:T(8,128)S(1)} collective-permute-done((f32[10,1,16,768]{3,2,1,0:T(8,128)S(1)}, f32[10,1,16,768]{3,2,1,0:T(8,128)S(1)}, u32[]{:S(2)}, u32[]{:S(2)}) %collective-permute-start.47) | collective-permute-done | bytes 491552 | tf_op jit(solution)/shard_map/ppermute | solution.py:25
  294.6 6.1 %multiply_select_fusion.1 = f32[8,8,16,768]{3,2,1,0:T(8,128)S(1)} fusion(f32[8,8,16,768]{3,2,1,0:T(8,128)S(1)} %convolution_add_fusion.1, f32[10,1,16,768]{3,2,1,0:T(8,128)S(1)} %collective-permute-done.47, f32[1,8,16,768]{3,2,1,0:T(8,128)S(1)} %collective-permute-done.45, f32[1,8,16,768]{3,2,1,0:T(8,128)S(1)} %collective-permute-done.44, ...), kind=kOutput, calls=%fused_computation.1 | convolution fusion | flops 73924608 | bytes 14414848 | tf_op jit(solution)/shard_map/kxyz,kv->xyzv/dot_general | solution.py:188
  300.8 11.2 %fusion.69 = f32[14,8,8,16]{3,0,2,1:T(8,128)S(1)} fusion(f32[8,8,16,768]{3,2,1,0:T(8,128)S(1)} %multiply_select_fusion.1, f32[14,768]{1,0:T(8,128)S(1)} %stack.29, f32[768]{0:T(1024)S(1)} %copy-done.6), kind=kOutput, calls=%fused_computation.579 | convolution fusion | flops 132131328 | bytes 3249152 | tf_op jit(solution)/shard_map/kv,xyzv->kxyz/dot_general | solution.py:173
  312.9 16.1 %psum.46 = f32[14,8,8,16]{3,2,1,0:T(8,128)} all-reduce(f32[14,8,8,16]{3,2,1,0:T(8,128)} %copy.15), channel_id=1, replica_groups=mesh['tx'=4,'ty'=2,'vel'=4] {'vel'}, use_global_device_ids=true, to_apply=%region_6.7 | all-reduce | flops 14336 | bytes 114688 | tf_op jit(solution)/shard_map/psum | solution.py:174
  329.7 3.8 collective-permute-start.48
  338.6 3.8 collective-permute-start.52
  346.8 2.2 collective-permute-done.55
  353.1 3.8 collective-permute-start.56
  366.2 2.8 collective-permute-start.60
  377.9 2.7 collective-permute-start.64
  386.5 22.9 %psum.47 = f32[]{:T(128)} all-reduce(f32[]{:T(128)} %slice_reduce_fusion), channel_id=1, replica_groups=mesh['tx'=4,'ty'=2,'vel'=4] {'tx','ty'}, use_global_device_ids=true, to_apply=%region_8.9 | all-reduce | flops 1 | bytes 8 | tf_op jit(solution)/shard_map/psum | solution.py:156
  412.3 2.8 convolution_add_fusion
  415.2 3.8 collective-permute-start.69
  419.0 5.9 %collective-permute-done.68 = f32[1,8,16,768]{3,2,1,0:T(8,128)S(1)} collective-permute-done((f32[1,8,16,768]{3,2,1,0:T(8,128)S(1)}, f32[1,8,16,768]{3,2,1,0:T(8,128)S(1)}, u32[]{:S(2)}, u32[]{:S(2)}) %collective-permute-start.68) | collective-permute-done | bytes 393248 | tf_op jit(solution)/shard_map/ppermute | solution.py:23
  424.9 2.4 collective-permute-done.69
  430.4 5.9 %collective-permute-done.70 = f32[10,1,16,768]{3,2,1,0:T(8,128)S(1)} collective-permute-done((f32[10,1,16,768]{3,2,1,0:T(8,128)S(1)}, f32[10,1,16,768]{3,2,1,0:T(8,128)S(1)}, u32[]{:S(2)}, u32[]{:S(2)}) %collective-permute-start.70) | collective-permute-done | bytes 491552 | tf_op jit(solution)/shard_map/ppermute | solution.py:23
  436.2 5.3 %collective-permute-done.71 = f32[10,1,16,768]{3,2,1,0:T(8,128)S(1)} collective-permute-done((f32[10,1,16,768]{3,2,1,0:T(8,128)S(1)}, f32[10,1,16,768]{3,2,1,0:T(8,128)S(1)}, u32[]{:S(2)}, u32[]{:S(2)}) %collective-permute-start.71) | collective-permute-done | bytes 491552 | tf_op jit(solution)/shard_map/ppermute | solution.py:25
  441.6 7.9 %multiply_select_fusion = f32[8,8,16,768]{3,2,1,0:T(8,128)} fusion(f32[8,8,16,768]{3,2,1,0:T(8,128)S(1)} %convolution_add_fusion, f32[10,1,16,768]{3,2,1,0:T(8,128)S(1)} %collective-permute-done.71, f32[1,8,16,768]{3,2,1,0:T(8,128)S(1)} %collective-permute-done.69, f32[1,8,16,768]{3,2,1,0:T(8,128)S(1)} %collective-permute-done.68, ...), kind=kOutput, calls=%fused_computation | convolution fusion | flops 73924608 | bytes 14414848 | tf_op jit(solution)/shard_map/kxyz,kv->xyzv/dot_general | solution.py:188
  (403 shorter events, 140.3 us)
Async XLA Ops:
  34.9 5.6 %collective-permute-start.1 = (f32[5,1,8,16]{3,2,1,0:T(8,128)S(1)}, f32[5,1,8,16]{3,2,1,0:T(8,128)S(1)}, u32[]{:S(2)}, u32[]{:S(2)}) collective-permute-start(f32[5,1,8,16]{3,2,1,0:T(8,128)S(1)} %get-tuple-element.84), channel_id=1, source_target_pairs={{0,8},{8,16},{16,24},{24,0},{1,9},{9,17},{17,25},{25,1},{2,10},{10... | collective-permute-start | bytes 7688 | tf_op jit(solution)/shard_map/ppermute | solution.py:23
  40.6 6.2 %collective-permute-start.3 = (f32[5,10,1,16]{3,2,1,0:T(1,128)S(1)}, f32[5,10,1,16]{3,2,1,0:T(1,128)S(1)}, u32[]{:S(2)}, u32[]{:S(2)}) collective-permute-start(f32[5,10,1,16]{3,2,1,0:T(1,128)S(1)} %get-tuple-element.162), channel_id=1, source_target_pairs={{0,4},{4,0},{1,5},{5,1},{2,6},{6,2},{3,7},{7,3},{8,12},{12,8},{9,1... | collective-permute-start | bytes 9608 | tf_op jit(solution)/shard_map/ppermute | solution.py:23
  42.2 4.6 %collective-permute-start.2 = (f32[5,10,1,16]{3,2,1,0:T(1,128)S(1)}, f32[5,10,1,16]{3,2,1,0:T(1,128)S(1)}, u32[]{:S(2)}, u32[]{:S(2)}) collective-permute-start(f32[5,10,1,16]{3,2,1,0:T(1,128)S(1)} %get-tuple-element.163), channel_id=1, source_target_pairs={{4,0},{0,4},{5,1},{1,5},{6,2},{2,6},{7,3},{3,7},{12,8},{8,12},{13,... | collective-permute-start | bytes 9608 | tf_op jit(solution)/shard_map/ppermute | solution.py:25
  42.7 6.1 %collective-permute-start.5 = (f32[13,1,8,16]{3,2,1,0:T(8,128)S(1)}, f32[13,1,8,16]{3,2,1,0:T(8,128)S(1)}, u32[]{:S(2)}, u32[]{:S(2)}) collective-permute-start(f32[13,1,8,16]{3,2,1,0:T(8,128)S(1)} %get-tuple-element.90), channel_id=1, source_target_pairs={{0,8},{8,16},{16,24},{24,0},{1,9},{9,17},{17,25},{25,1},{2,10},{10... | collective-permute-start | bytes 19976 | tf_op jit(solution)/shard_map/ppermute | solution.py:23
  44.1 4.9 %collective-permute-start.4 = (f32[13,1,8,16]{3,2,1,0:T(8,128)S(1)}, f32[13,1,8,16]{3,2,1,0:T(8,128)S(1)}, u32[]{:S(2)}, u32[]{:S(2)}) collective-permute-start(f32[13,1,8,16]{3,2,1,0:T(8,128)S(1)} %get-tuple-element.91), channel_id=1, source_target_pairs={{8,0},{16,8},{24,16},{0,24},{9,1},{17,9},{25,17},{1,25},{10,2},{18... | collective-permute-start | bytes 19976 | tf_op jit(solution)/shard_map/ppermute | solution.py:25
  57.3 5.6 %collective-permute-start.9 = (f32[5,1,8,16]{3,2,1,0:T(8,128)S(1)}, f32[5,1,8,16]{3,2,1,0:T(8,128)S(1)}, u32[]{:S(2)}, u32[]{:S(2)}) collective-permute-start(f32[5,1,8,16]{3,2,1,0:T(8,128)S(1)} %get-tuple-element.184), channel_id=1, source_target_pairs={{0,8},{8,16},{16,24},{24,0},{1,9},{9,17},{17,25},{25,1},{2,10},{10... | collective-permute-start | bytes 7688 | tf_op jit(solution)/shard_map/ppermute | solution.py:23
  68.7 5.8 %collective-permute-start.13 = (f32[5,1,8,16]{3,2,1,0:T(8,128)S(1)}, f32[5,1,8,16]{3,2,1,0:T(8,128)S(1)}, u32[]{:S(2)}, u32[]{:S(2)}) collective-permute-start(f32[5,1,8,16]{3,2,1,0:T(8,128)S(1)} %get-tuple-element.182), channel_id=1, source_target_pairs={{0,8},{8,16},{16,24},{24,0},{1,9},{9,17},{17,25},{25,1},{2,10},{10... | collective-permute-start | bytes 7688 | tf_op jit(solution)/shard_map/ppermute | solution.py:23
  80.9 5.7 %collective-permute-start.17 = (f32[5,1,8,16]{3,2,1,0:T(8,128)S(1)}, f32[5,1,8,16]{3,2,1,0:T(8,128)S(1)}, u32[]{:S(2)}, u32[]{:S(2)}) collective-permute-start(f32[5,1,8,16]{3,2,1,0:T(8,128)S(1)} %get-tuple-element.180), channel_id=1, source_target_pairs={{0,8},{8,16},{16,24},{24,0},{1,9},{9,17},{17,25},{25,1},{2,10},{10... | collective-permute-start | bytes 7688 | tf_op jit(solution)/shard_map/ppermute | solution.py:23
  86.7 25.9 %collective-permute-start.19 = (f32[5,10,1,16]{3,2,1,0:T(1,128)S(1)}, f32[5,10,1,16]{3,2,1,0:T(1,128)S(1)}, u32[]{:S(2)}, u32[]{:S(2)}) collective-permute-start(f32[5,10,1,16]{3,2,1,0:T(1,128)S(1)} %get-tuple-element.150), channel_id=1, source_target_pairs={{0,4},{4,0},{1,5},{5,1},{2,6},{6,2},{3,7},{7,3},{8,12},{12,8},{9,1... | collective-permute-start | bytes 9608 | tf_op jit(solution)/shard_map/ppermute | solution.py:23
  87.4 25.2 %collective-permute-start.18 = (f32[5,10,1,16]{3,2,1,0:T(1,128)S(1)}, f32[5,10,1,16]{3,2,1,0:T(1,128)S(1)}, u32[]{:S(2)}, u32[]{:S(2)}) collective-permute-start(f32[5,10,1,16]{3,2,1,0:T(1,128)S(1)} %get-tuple-element.151), channel_id=1, source_target_pairs={{4,0},{0,4},{5,1},{1,5},{6,2},{2,6},{7,3},{3,7},{12,8},{8,12},{13,... | collective-permute-start | bytes 9608 | tf_op jit(solution)/shard_map/ppermute | solution.py:25
  117.6 9.7 %collective-permute-start.20 = (f32[1,8,16,768]{3,2,1,0:T(8,128)S(1)}, f32[1,8,16,768]{3,2,1,0:T(8,128)S(1)}, u32[]{:S(2)}, u32[]{:S(2)}) collective-permute-start(f32[1,8,16,768]{3,2,1,0:T(8,128)S(1)} %get-tuple-element.60), channel_id=1, source_target_pairs={{0,8},{8,16},{16,24},{24,0},{1,9},{9,17},{17,25},{25,1},{2,10},{10... | collective-permute-start | bytes 1179656 | tf_op jit(solution)/shard_map/ppermute | solution.py:23
  117.6 12.4 %collective-permute-start.21 = (f32[1,8,16,768]{3,2,1,0:T(8,128)S(1)}, f32[1,8,16,768]{3,2,1,0:T(8,128)S(1)}, u32[]{:S(2)}, u32[]{:S(2)}) collective-permute-start(f32[1,8,16,768]{3,2,1,0:T(8,128)S(1)} %get-tuple-element.61), channel_id=1, source_target_pairs={{8,0},{16,8},{24,16},{0,24},{9,1},{17,9},{25,17},{1,25},{10,2},{18... | collective-permute-start | bytes 1179656 | tf_op jit(solution)/shard_map/ppermute | solution.py:25
  130.1 8.9 %collective-permute-start.22 = (f32[10,1,16,768]{3,2,1,0:T(8,128)S(1)}, f32[10,1,16,768]{3,2,1,0:T(8,128)S(1)}, u32[]{:S(2)}, u32[]{:S(2)}) collective-permute-start(f32[10,1,16,768]{3,2,1,0:T(8,128)S(1)} %get-tuple-element.42), channel_id=1, source_target_pairs={{0,4},{4,0},{1,5},{5,1},{2,6},{6,2},{3,7},{7,3},{8,12},{12,8},{9,1... | collective-permute-start | bytes 1474568 | tf_op jit(solution)/shard_map/ppermute | solution.py:23
  130.2 14.1 %collective-permute-start.23 = (f32[10,1,16,768]{3,2,1,0:T(8,128)S(1)}, f32[10,1,16,768]{3,2,1,0:T(8,128)S(1)}, u32[]{:S(2)}, u32[]{:S(2)}) collective-permute-start(f32[10,1,16,768]{3,2,1,0:T(8,128)S(1)} %get-tuple-element.43), channel_id=1, source_target_pairs={{4,0},{0,4},{5,1},{1,5},{6,2},{2,6},{7,3},{3,7},{12,8},{8,12},{13,... | collective-permute-start | bytes 1474568 | tf_op jit(solution)/shard_map/ppermute | solution.py:25
  179.5 6.7 %collective-permute-start.25 = (f32[5,1,8,16]{3,2,1,0:T(8,128)S(1)}, f32[5,1,8,16]{3,2,1,0:T(8,128)S(1)}, u32[]{:S(2)}, u32[]{:S(2)}) collective-permute-start(f32[5,1,8,16]{3,2,1,0:T(8,128)S(1)} %get-tuple-element.82), channel_id=1, source_target_pairs={{0,8},{8,16},{16,24},{24,0},{1,9},{9,17},{17,25},{25,1},{2,10},{10... | collective-permute-start | bytes 7688 | tf_op jit(solution)/shard_map/ppermute | solution.py:23
  180.5 5.6 %collective-permute-start.24 = (f32[5,1,8,16]{3,2,1,0:T(8,128)S(1)}, f32[5,1,8,16]{3,2,1,0:T(8,128)S(1)}, u32[]{:S(2)}, u32[]{:S(2)}) collective-permute-start(f32[5,1,8,16]{3,2,1,0:T(8,128)S(1)} %get-tuple-element.83), channel_id=1, source_target_pairs={{8,0},{16,8},{24,16},{0,24},{9,1},{17,9},{25,17},{1,25},{10,2},{18... | collective-permute-start | bytes 7688 | tf_op jit(solution)/shard_map/ppermute | solution.py:25
  186.2 6.0 %collective-permute-start.27 = (f32[5,10,1,16]{3,2,1,0:T(1,128)S(1)}, f32[5,10,1,16]{3,2,1,0:T(1,128)S(1)}, u32[]{:S(2)}, u32[]{:S(2)}) collective-permute-start(f32[5,10,1,16]{3,2,1,0:T(1,128)S(1)} %get-tuple-element.146), channel_id=1, source_target_pairs={{0,4},{4,0},{1,5},{5,1},{2,6},{6,2},{3,7},{7,3},{8,12},{12,8},{9,1... | collective-permute-start | bytes 9608 | tf_op jit(solution)/shard_map/ppermute | solution.py:23
  186.3 5.9 %collective-permute-start.26 = (f32[5,10,1,16]{3,2,1,0:T(1,128)S(1)}, f32[5,10,1,16]{3,2,1,0:T(1,128)S(1)}, u32[]{:S(2)}, u32[]{:S(2)}) collective-permute-start(f32[5,10,1,16]{3,2,1,0:T(1,128)S(1)} %get-tuple-element.147), channel_id=1, source_target_pairs={{4,0},{0,4},{5,1},{1,5},{6,2},{2,6},{7,3},{3,7},{12,8},{8,12},{13,... | collective-permute-start | bytes 9608 | tf_op jit(solution)/shard_map/ppermute | solution.py:25
  188.3 6.0 %collective-permute-start.29 = (f32[13,1,8,16]{3,2,1,0:T(8,128)S(1)}, f32[13,1,8,16]{3,2,1,0:T(8,128)S(1)}, u32[]{:S(2)}, u32[]{:S(2)}) collective-permute-start(f32[13,1,8,16]{3,2,1,0:T(8,128)S(1)} %get-tuple-element.88), channel_id=1, source_target_pairs={{0,8},{8,16},{16,24},{24,0},{1,9},{9,17},{17,25},{25,1},{2,10},{10... | collective-permute-start | bytes 19976 | tf_op jit(solution)/shard_map/ppermute | solution.py:23
  188.4 6.0 %collective-permute-start.28 = (f32[13,1,8,16]{3,2,1,0:T(8,128)S(1)}, f32[13,1,8,16]{3,2,1,0:T(8,128)S(1)}, u32[]{:S(2)}, u32[]{:S(2)}) collective-permute-start(f32[13,1,8,16]{3,2,1,0:T(8,128)S(1)} %get-tuple-element.89), channel_id=1, source_target_pairs={{8,0},{16,8},{24,16},{0,24},{9,1},{17,9},{25,17},{1,25},{10,2},{18... | collective-permute-start | bytes 19976 | tf_op jit(solution)/shard_map/ppermute | solution.py:25
  194.6 4.9 %collective-permute-start.30 = (f32[13,10,1,16]{3,2,1,0:T(1,128)S(1)}, f32[13,10,1,16]{3,2,1,0:T(1,128)S(1)}, u32[]{:S(2)}, u32[]{:S(2)}) collective-permute-start(f32[13,10,1,16]{3,2,1,0:T(1,128)S(1)} %get-tuple-element.75), channel_id=1, source_target_pairs={{4,0},{0,4},{5,1},{1,5},{6,2},{2,6},{7,3},{3,7},{12,8},{8,12},{13,... | collective-permute-start | bytes 24968 | tf_op jit(solution)/shard_map/ppermute | solution.py:25
  202.8 5.6 %collective-permute-start.33 = (f32[5,1,8,16]{3,2,1,0:T(8,128)S(1)}, f32[5,1,8,16]{3,2,1,0:T(8,128)S(1)}, u32[]{:S(2)}, u32[]{:S(2)}) collective-permute-start(f32[5,1,8,16]{3,2,1,0:T(8,128)S(1)} %get-tuple-element.176), channel_id=1, source_target_pairs={{0,8},{8,16},{16,24},{24,0},{1,9},{9,17},{17,25},{25,1},{2,10},{10... | collective-permute-start | bytes 7688 | tf_op jit(solution)/shard_map/ppermute | solution.py:23
  202.9 5.6 %collective-permute-start.32 = (f32[5,1,8,16]{3,2,1,0:T(8,128)S(1)}, f32[5,1,8,16]{3,2,1,0:T(8,128)S(1)}, u32[]{:S(2)}, u32[]{:S(2)}) collective-permute-start(f32[5,1,8,16]{3,2,1,0:T(8,128)S(1)} %get-tuple-element.177), channel_id=1, source_target_pairs={{8,0},{16,8},{24,16},{0,24},{9,1},{17,9},{25,17},{1,25},{10,2},{18... | collective-permute-start | bytes 7688 | tf_op jit(solution)/shard_map/ppermute | solution.py:25
  214.8 5.7 %collective-permute-start.37 = (f32[5,1,8,16]{3,2,1,0:T(8,128)S(1)}, f32[5,1,8,16]{3,2,1,0:T(8,128)S(1)}, u32[]{:S(2)}, u32[]{:S(2)}) collective-permute-start(f32[5,1,8,16]{3,2,1,0:T(8,128)S(1)} %get-tuple-element.174), channel_id=1, source_target_pairs={{0,8},{8,16},{16,24},{24,0},{1,9},{9,17},{17,25},{25,1},{2,10},{10... | collective-permute-start | bytes 7688 | tf_op jit(solution)/shard_map/ppermute | solution.py:23
  226.5 5.7 %collective-permute-start.41 = (f32[5,1,8,16]{3,2,1,0:T(8,128)S(1)}, f32[5,1,8,16]{3,2,1,0:T(8,128)S(1)}, u32[]{:S(2)}, u32[]{:S(2)}) collective-permute-start(f32[5,1,8,16]{3,2,1,0:T(8,128)S(1)} %get-tuple-element.172), channel_id=1, source_target_pairs={{0,8},{8,16},{16,24},{24,0},{1,9},{9,17},{17,25},{25,1},{2,10},{10... | collective-permute-start | bytes 7688 | tf_op jit(solution)/shard_map/ppermute | solution.py:23
  232.8 26.8 %collective-permute-start.43 = (f32[5,10,1,16]{3,2,1,0:T(1,128)}, f32[5,10,1,16]{3,2,1,0:T(1,128)}, u32[]{:S(2)}, u32[]{:S(2)}) collective-permute-start(f32[5,10,1,16]{3,2,1,0:T(1,128)} %get-tuple-element.134), channel_id=1, source_target_pairs={{0,4},{4,0},{1,5},{5,1},{2,6},{6,2},{3,7},{7,3},{8,12},{12,8},{9,1... | collective-permute-start | bytes 9608 | tf_op jit(solution)/shard_map/ppermute | solution.py:23
  234.2 25.5 %collective-permute-start.42 = (f32[5,10,1,16]{3,2,1,0:T(1,128)}, f32[5,10,1,16]{3,2,1,0:T(1,128)}, u32[]{:S(2)}, u32[]{:S(2)}) collective-permute-start(f32[5,10,1,16]{3,2,1,0:T(1,128)} %get-tuple-element.135), channel_id=1, source_target_pairs={{4,0},{0,4},{5,1},{1,5},{6,2},{2,6},{7,3},{3,7},{12,8},{8,12},{13,... | collective-permute-start | bytes 9608 | tf_op jit(solution)/shard_map/ppermute | solution.py:25
  267.8 9.7 %collective-permute-start.44 = (f32[1,8,16,768]{3,2,1,0:T(8,128)S(1)}, f32[1,8,16,768]{3,2,1,0:T(8,128)S(1)}, u32[]{:S(2)}, u32[]{:S(2)}) collective-permute-start(f32[1,8,16,768]{3,2,1,0:T(8,128)S(1)} %get-tuple-element.54), channel_id=1, source_target_pairs={{0,8},{8,16},{16,24},{24,0},{1,9},{9,17},{17,25},{25,1},{2,10},{10... | collective-permute-start | bytes 1179656 | tf_op jit(solution)/shard_map/ppermute | solution.py:23
  267.9 12.4 %collective-permute-start.45 = (f32[1,8,16,768]{3,2,1,0:T(8,128)S(1)}, f32[1,8,16,768]{3,2,1,0:T(8,128)S(1)}, u32[]{:S(2)}, u32[]{:S(2)}) collective-permute-start(f32[1,8,16,768]{3,2,1,0:T(8,128)S(1)} %get-tuple-element.55), channel_id=1, source_target_pairs={{8,0},{16,8},{24,16},{0,24},{9,1},{17,9},{25,17},{1,25},{10,2},{18... | collective-permute-start | bytes 1179656 | tf_op jit(solution)/shard_map/ppermute | solution.py:25
  280.4 8.9 %collective-permute-start.46 = (f32[10,1,16,768]{3,2,1,0:T(8,128)S(1)}, f32[10,1,16,768]{3,2,1,0:T(8,128)S(1)}, u32[]{:S(2)}, u32[]{:S(2)}) collective-permute-start(f32[10,1,16,768]{3,2,1,0:T(8,128)S(1)} %get-tuple-element.40), channel_id=1, source_target_pairs={{0,4},{4,0},{1,5},{5,1},{2,6},{6,2},{3,7},{7,3},{8,12},{12,8},{9,1... | collective-permute-start | bytes 1474568 | tf_op jit(solution)/shard_map/ppermute | solution.py:23
  280.5 14.1 %collective-permute-start.47 = (f32[10,1,16,768]{3,2,1,0:T(8,128)S(1)}, f32[10,1,16,768]{3,2,1,0:T(8,128)S(1)}, u32[]{:S(2)}, u32[]{:S(2)}) collective-permute-start(f32[10,1,16,768]{3,2,1,0:T(8,128)S(1)} %get-tuple-element.41), channel_id=1, source_target_pairs={{4,0},{0,4},{5,1},{1,5},{6,2},{2,6},{7,3},{3,7},{12,8},{8,12},{13,... | collective-permute-start | bytes 1474568 | tf_op jit(solution)/shard_map/ppermute | solution.py:25
  329.7 6.7 %collective-permute-start.49 = (f32[5,1,8,16]{3,2,1,0:T(8,128)S(1)}, f32[5,1,8,16]{3,2,1,0:T(8,128)S(1)}, u32[]{:S(2)}, u32[]{:S(2)}) collective-permute-start(f32[5,1,8,16]{3,2,1,0:T(8,128)S(1)} %get-tuple-element.80), channel_id=1, source_target_pairs={{0,8},{8,16},{16,24},{24,0},{1,9},{9,17},{17,25},{25,1},{2,10},{10... | collective-permute-start | bytes 7688 | tf_op jit(solution)/shard_map/ppermute | solution.py:23
  329.7 6.7 %collective-permute-start.48 = (f32[5,1,8,16]{3,2,1,0:T(8,128)S(1)}, f32[5,1,8,16]{3,2,1,0:T(8,128)S(1)}, u32[]{:S(2)}, u32[]{:S(2)}) collective-permute-start(f32[5,1,8,16]{3,2,1,0:T(8,128)S(1)} %get-tuple-element.81), channel_id=1, source_target_pairs={{8,0},{16,8},{24,16},{0,24},{9,1},{17,9},{25,17},{1,25},{10,2},{18... | collective-permute-start | bytes 7688 | tf_op jit(solution)/shard_map/ppermute | solution.py:25
  336.5 6.0 %collective-permute-start.51 = (f32[5,10,1,16]{3,2,1,0:T(1,128)S(1)}, f32[5,10,1,16]{3,2,1,0:T(1,128)S(1)}, u32[]{:S(2)}, u32[]{:S(2)}) collective-permute-start(f32[5,10,1,16]{3,2,1,0:T(1,128)S(1)} %get-tuple-element.130), channel_id=1, source_target_pairs={{0,4},{4,0},{1,5},{5,1},{2,6},{6,2},{3,7},{7,3},{8,12},{12,8},{9,1... | collective-permute-start | bytes 9608 | tf_op jit(solution)/shard_map/ppermute | solution.py:23
  336.5 5.9 %collective-permute-start.50 = (f32[5,10,1,16]{3,2,1,0:T(1,128)S(1)}, f32[5,10,1,16]{3,2,1,0:T(1,128)S(1)}, u32[]{:S(2)}, u32[]{:S(2)}) collective-permute-start(f32[5,10,1,16]{3,2,1,0:T(1,128)S(1)} %get-tuple-element.131), channel_id=1, source_target_pairs={{4,0},{0,4},{5,1},{1,5},{6,2},{2,6},{7,3},{3,7},{12,8},{8,12},{13,... | collective-permute-start | bytes 9608 | tf_op jit(solution)/shard_map/ppermute | solution.py:25
  338.6 6.0 %collective-permute-start.53 = (f32[13,1,8,16]{3,2,1,0:T(8,128)S(1)}, f32[13,1,8,16]{3,2,1,0:T(8,128)S(1)}, u32[]{:S(2)}, u32[]{:S(2)}) collective-permute-start(f32[13,1,8,16]{3,2,1,0:T(8,128)S(1)} %get-tuple-element.86), channel_id=1, source_target_pairs={{0,8},{8,16},{16,24},{24,0},{1,9},{9,17},{17,25},{25,1},{2,10},{10... | collective-permute-start | bytes 19976 | tf_op jit(solution)/shard_map/ppermute | solution.py:23
  338.6 6.0 %collective-permute-start.52 = (f32[13,1,8,16]{3,2,1,0:T(8,128)S(1)}, f32[13,1,8,16]{3,2,1,0:T(8,128)S(1)}, u32[]{:S(2)}, u32[]{:S(2)}) collective-permute-start(f32[13,1,8,16]{3,2,1,0:T(8,128)S(1)} %get-tuple-element.87), channel_id=1, source_target_pairs={{8,0},{16,8},{24,16},{0,24},{9,1},{17,9},{25,17},{1,25},{10,2},{18... | collective-permute-start | bytes 19976 | tf_op jit(solution)/shard_map/ppermute | solution.py:25
  344.8 4.9 %collective-permute-start.54 = (f32[13,10,1,16]{3,2,1,0:T(1,128)S(1)}, f32[13,10,1,16]{3,2,1,0:T(1,128)S(1)}, u32[]{:S(2)}, u32[]{:S(2)}) collective-permute-start(f32[13,10,1,16]{3,2,1,0:T(1,128)S(1)} %get-tuple-element.71), channel_id=1, source_target_pairs={{4,0},{0,4},{5,1},{1,5},{6,2},{2,6},{7,3},{3,7},{12,8},{8,12},{13,... | collective-permute-start | bytes 24968 | tf_op jit(solution)/shard_map/ppermute | solution.py:25
  353.1 5.6 %collective-permute-start.57 = (f32[5,1,8,16]{3,2,1,0:T(8,128)S(1)}, f32[5,1,8,16]{3,2,1,0:T(8,128)S(1)}, u32[]{:S(2)}, u32[]{:S(2)}) collective-permute-start(f32[5,1,8,16]{3,2,1,0:T(8,128)S(1)} %get-tuple-element.168), channel_id=1, source_target_pairs={{0,8},{8,16},{16,24},{24,0},{1,9},{9,17},{17,25},{25,1},{2,10},{10... | collective-permute-start | bytes 7688 | tf_op jit(solution)/shard_map/ppermute | solution.py:23
  353.1 5.6 %collective-permute-start.56 = (f32[5,1,8,16]{3,2,1,0:T(8,128)S(1)}, f32[5,1,8,16]{3,2,1,0:T(8,128)S(1)}, u32[]{:S(2)}, u32[]{:S(2)}) collective-permute-start(f32[5,1,8,16]{3,2,1,0:T(8,128)S(1)} %get-tuple-element.169), channel_id=1, source_target_pairs={{8,0},{16,8},{24,16},{0,24},{9,1},{17,9},{25,17},{1,25},{10,2},{18... | collective-permute-start | bytes 7688 | tf_op jit(solution)/shard_map/ppermute | solution.py:25
  365.1 5.7 %collective-permute-start.61 = (f32[5,1,8,16]{3,2,1,0:T(8,128)S(1)}, f32[5,1,8,16]{3,2,1,0:T(8,128)S(1)}, u32[]{:S(2)}, u32[]{:S(2)}) collective-permute-start(f32[5,1,8,16]{3,2,1,0:T(8,128)S(1)} %get-tuple-element.166), channel_id=1, source_target_pairs={{0,8},{8,16},{16,24},{24,0},{1,9},{9,17},{17,25},{25,1},{2,10},{10... | collective-permute-start | bytes 7688 | tf_op jit(solution)/shard_map/ppermute | solution.py:23
  376.8 5.6 %collective-permute-start.65 = (f32[5,1,8,16]{3,2,1,0:T(8,128)S(1)}, f32[5,1,8,16]{3,2,1,0:T(8,128)S(1)}, u32[]{:S(2)}, u32[]{:S(2)}) collective-permute-start(f32[5,1,8,16]{3,2,1,0:T(8,128)S(1)} %get-tuple-element.164), channel_id=1, source_target_pairs={{0,8},{8,16},{16,24},{24,0},{1,9},{9,17},{17,25},{25,1},{2,10},{10... | collective-permute-start | bytes 7688 | tf_op jit(solution)/shard_map/ppermute | solution.py:23
  383.1 27.1 %collective-permute-start.67 = (f32[5,10,1,16]{3,2,1,0:T(1,128)}, f32[5,10,1,16]{3,2,1,0:T(1,128)S(1)}, u32[]{:S(2)}, u32[]{:S(2)}) collective-permute-start(f32[5,10,1,16]{3,2,1,0:T(1,128)} %get-tuple-element.118), channel_id=1, source_target_pairs={{0,4},{4,0},{1,5},{5,1},{2,6},{6,2},{3,7},{7,3},{8,12},{12,8},{9,1... | collective-permute-start | bytes 9608 | tf_op jit(solution)/shard_map/ppermute | solution.py:23
  384.4 25.7 %collective-permute-start.66 = (f32[5,10,1,16]{3,2,1,0:T(1,128)}, f32[5,10,1,16]{3,2,1,0:T(1,128)S(1)}, u32[]{:S(2)}, u32[]{:S(2)}) collective-permute-start(f32[5,10,1,16]{3,2,1,0:T(1,128)} %get-tuple-element.119), channel_id=1, source_target_pairs={{4,0},{0,4},{5,1},{1,5},{6,2},{2,6},{7,3},{3,7},{12,8},{8,12},{13,... | collective-permute-start | bytes 9608 | tf_op jit(solution)/shard_map/ppermute | solution.py:25
  415.2 9.7 %collective-permute-start.68 = (f32[1,8,16,768]{3,2,1,0:T(8,128)S(1)}, f32[1,8,16,768]{3,2,1,0:T(8,128)S(1)}, u32[]{:S(2)}, u32[]{:S(2)}) collective-permute-start(f32[1,8,16,768]{3,2,1,0:T(8,128)S(1)} %get-tuple-element.48), channel_id=1, source_target_pairs={{0,8},{8,16},{16,24},{24,0},{1,9},{9,17},{17,25},{25,1},{2,10},{10... | collective-permute-start | bytes 1179656 | tf_op jit(solution)/shard_map/ppermute | solution.py:23
  415.2 12.0 %collective-permute-start.69 = (f32[1,8,16,768]{3,2,1,0:T(8,128)S(1)}, f32[1,8,16,768]{3,2,1,0:T(8,128)S(1)}, u32[]{:S(2)}, u32[]{:S(2)}) collective-permute-start(f32[1,8,16,768]{3,2,1,0:T(8,128)S(1)} %get-tuple-element.49), channel_id=1, source_target_pairs={{8,0},{16,8},{24,16},{0,24},{9,1},{17,9},{25,17},{1,25},{10,2},{18... | collective-permute-start | bytes 1179656 | tf_op jit(solution)/shard_map/ppermute | solution.py:25
  427.3 8.9 %collective-permute-start.70 = (f32[10,1,16,768]{3,2,1,0:T(8,128)S(1)}, f32[10,1,16,768]{3,2,1,0:T(8,128)S(1)}, u32[]{:S(2)}, u32[]{:S(2)}) collective-permute-start(f32[10,1,16,768]{3,2,1,0:T(8,128)S(1)} %get-tuple-element.38), channel_id=1, source_target_pairs={{0,4},{4,0},{1,5},{5,1},{2,6},{6,2},{3,7},{7,3},{8,12},{12,8},{9,1... | collective-permute-start | bytes 1474568 | tf_op jit(solution)/shard_map/ppermute | solution.py:23
  427.4 14.1 %collective-permute-start.71 = (f32[10,1,16,768]{3,2,1,0:T(8,128)S(1)}, f32[10,1,16,768]{3,2,1,0:T(8,128)S(1)}, u32[]{:S(2)}, u32[]{:S(2)}) collective-permute-start(f32[10,1,16,768]{3,2,1,0:T(8,128)S(1)} %get-tuple-element.39), channel_id=1, source_target_pairs={{4,0},{0,4},{5,1},{1,5},{6,2},{2,6},{7,3},{3,7},{12,8},{8,12},{13,... | collective-permute-start | bytes 1474568 | tf_op jit(solution)/shard_map/ppermute | solution.py:25
  (59 other events, 877.1 us)
where the time goes:
time: 457 us; the launch traced here: 450 us
  blocking collectives  117 us (26%)
  starting transfers between devices  109 us (24%)
  waiting for transfers between devices  106 us (23%)
  matrix products  63.9 us (14%)
  other arithmetic  31.8 us (7%)
  local copies, waits for them, and re-layouts  17.1 us (4%)
  between operations  5.41 us (1%)
    ppermute x36, starting transfers between devices, padded_2(): lax.ppermute(head, axis, [((i + 1) % count, i) for i in range(count)])  82.2 us
    ppermute x36, waiting for transfers between devices, padded_2(): lax.ppermute(tail, axis, [(i, (i + 1) % count) for i in range(count)])  72.4 us
    psum x3, blocking collectives, total_mass(): summed = lax.psum(local_sum, ('tx', 'ty'))  67.4 us
    psum x3, blocking collectives, on_device(): moments = lax.psum(local_moments, 'vel')  49.5 us
    dot_general x3, matrix products, on_device(): jnp.einsum('kv,xyzv->kxyz', moment_rows, distribution, precision=highest)  35.4 us
    ppermute x36, waiting for transfers between devices, padded_2(): lax.ppermute(head, axis, [((i + 1) % count, i) for i in range(count)])  33.4 us
    ppermute x36, starting transfers between devices, padded_2(): lax.ppermute(tail, axis, [(i, (i + 1) % count) for i in range(count)])  26.5 us
    dot_general x3, matrix products, on_device(): jnp.einsum('kxyz,kv->xyzv', macro_state, rows, precision=highest)  20.1 us
  transfers between devices with their start and end apart: 72, of which 44 were waited for; matrix products, arithmetic and copies ran while one was open for 3% of the time, Pallas kernels for 0%

commit v1 on v0

--- a/solution.py
+++ b/solution.py
@@ -171,7 +171,10 @@
     macro_state = None
     for iteration in range(ITERS):
         local_moments = jnp.einsum("kv,xyzv->kxyz", moment_rows, distribution, precision=highest)
-        moments = lax.psum(local_moments, "vel")
+        n_dev, moments = (lax.axis_size("vel"), local_moments)
+        for far in [1 << k for k in range(n_dev.bit_length() - 1)]:
+            route = [(i_2, i_2 ^ far) for i_2 in range(n_dev)]
+            moments = moments + lax.ppermute(moments, "vel", route)
         kinetic_state = moments[0:5]
         fields = jnp.concatenate([moments[5:14], moments[1:5]])
         mass_total = total_mass(jnp.sum(kinetic_state[0]))

time: 457 us -> 443 us (0.969)
  blocking collectives: 117 us -> 67.2 us
  waiting for transfers between devices: 106 us -> 146 us
  local copies, waits for them, and re-layouts: 17.1 us -> 8.55 us
  starting transfers between devices: 109 us -> 116 us
    psum x3 -> x0, blocking collectives: 49.5 us -> none  [on_device(): moments = lax.psum(local_moments, 'vel')]
    ppermute x0 -> x6, waiting for transfers between devices: none -> 38 us  [on_device(): moments = moments + lax.ppermute(moments, 'vel', route)]
    ppermute x0 -> x6, starting transfers between devices: none -> 6.72 us  [on_device(): moments = moments + lax.ppermute(moments, 'vel', route)]
    ppermute x36, starting transfers between devices: 26.5 us -> 31.6 us  [padded_2(): lax.ppermute(tail, axis, [(i, (i + 1) % count) for i in range(count)])]
  transfers between devices with their start and end apart: 72 -> 78, of which waited for: 44 -> 52; matrix products, arithmetic and copies ran while one was open for 3% -> 2% of each run, Pallas kernels for 0% -> 0%
where the time goes in v1:
time: 443 us; the launch traced here: 436 us
  waiting for transfers between devices  146 us (33%)
  starting transfers between devices  116 us (26%)
  blocking collectives  67.2 us (15%)
  matrix products  63.9 us (14%)
  other arithmetic  29 us (7%)
  local copies, waits for them, and re-layouts  8.55 us (2%)
  between operations  5.41 us (1%)
    ppermute x36, starting transfers between devices, padded_2(): lax.ppermute(head, axis, [((i + 1) % count, i) for i in range(count)])  77.9 us
    ppermute x36, waiting for transfers between devices, padded_2(): lax.ppermute(tail, axis, [(i, (i + 1) % count) for i in range(count)])  75.1 us
    psum x3, blocking collectives, total_mass(): summed = lax.psum(local_sum, ('tx', 'ty'))  67.2 us
    ppermute x6, waiting for transfers between devices, on_device(): moments = moments + lax.ppermute(moments, 'vel', route)  38 us
    dot_general x3, matrix products, on_device(): jnp.einsum('kv,xyzv->kxyz', moment_rows, distribution, precision=highest)  35.4 us
    ppermute x36, waiting for transfers between devices, padded_2(): lax.ppermute(head, axis, [((i + 1) % count, i) for i in range(count)])  32.9 us
    ppermute x36, starting transfers between devices, padded_2(): lax.ppermute(tail, axis, [(i, (i + 1) % count) for i in range(count)])  31.6 us
    dot_general x3, matrix products, on_device(): jnp.einsum('kxyz,kv->xyzv', macro_state, rows, precision=highest)  20.1 us
  transfers between devices with their start and end apart: 78, of which 52 were waited for; matrix products, arithmetic and copies ran while one was open for 2% of the time, Pallas kernels for 0%

profile of v1, /device:TPU:0, one launch (start us, length us, event | category | flops | bytes accessed | tf_op | source)
XLA Modules:
  0.0 436.3 jit_solution(3835065429991033864)
XLA Ops:
  4.4 12.9 %fusion.73 = f32[14,8,8,16]{3,0,2,1:T(8,128)S(1)} fusion(f32[8,8,16,768]{3,2,1,0:T(8,128)} %param.6, f32[14,768]{1,0:T(8,128)S(1)} %stack.29, f32[768]{0:T(1024)S(1)} %broadcast_multiply_fusion), kind=kOutput, calls=%fused_computation.583 | convolution fusion | flops 132131328 | bytes 3249152 | tf_op jit(solution)/shard_map/kv,xyzv->kxyz/dot_general | solution.py:173
  19.7 2.9 collective-permute-start.1
  22.6 10.8 %collective-permute-done.1 = f32[14,8,8,16]{3,2,1,0:T(8,128)S(1)} collective-permute-done((f32[14,8,8,16]{3,2,1,0:T(8,128)S(1)}, f32[14,8,8,16]{3,2,1,0:T(8,128)S(1)}, u32[]{:S(2)}, u32[]{:S(2)}) %collective-permute-start.1) | collective-permute-done | bytes 57376 | tf_op jit(solution)/shard_map/ppermute | solution.py:177
  42.9 2.6 collective-permute-start.6
  50.0 2.2 collective-permute-done.9
  57.2 2.8 collective-permute-start.10
  68.8 2.7 collective-permute-start.14
  81.2 2.4 collective-permute-start.18
  88.1 22.0 %psum.21 = f32[]{:T(128)} all-reduce(f32[]{:T(128)} %slice_reduce_fusion.2), channel_id=1, replica_groups=mesh['tx'=4,'ty'=2,'vel'=4] {'tx','ty'}, use_global_device_ids=true, to_apply=%region_1.0 | all-reduce | flops 1 | bytes 8 | tf_op jit(solution)/shard_map/psum | solution.py:156
  112.8 2.8 convolution_add_fusion.2
  115.7 4.2 collective-permute-start.23
  120.1 5.3 %collective-permute-done.22 = f32[1,8,16,768]{3,2,1,0:T(8,128)S(1)} collective-permute-done((f32[1,8,16,768]{3,2,1,0:T(8,128)S(1)}, f32[1,8,16,768]{3,2,1,0:T(8,128)S(1)}, u32[]{:S(2)}, u32[]{:S(2)}) %collective-permute-start.22) | collective-permute-done | bytes 393248 | tf_op jit(solution)/shard_map/ppermute | solution.py:23
  125.4 2.8 collective-permute-done.23
  131.2 5.9 %collective-permute-done.24 = f32[10,1,16,768]{3,2,1,0:T(8,128)S(1)} collective-permute-done((f32[10,1,16,768]{3,2,1,0:T(8,128)S(1)}, f32[10,1,16,768]{3,2,1,0:T(8,128)S(1)}, u32[]{:S(2)}, u32[]{:S(2)}) %collective-permute-start.24) | collective-permute-done | bytes 491552 | tf_op jit(solution)/shard_map/ppermute | solution.py:23
  137.1 5.3 %collective-permute-done.25 = f32[10,1,16,768]{3,2,1,0:T(8,128)S(1)} collective-permute-done((f32[10,1,16,768]{3,2,1,0:T(8,128)S(1)}, f32[10,1,16,768]{3,2,1,0:T(8,128)S(1)}, u32[]{:S(2)}, u32[]{:S(2)}) %collective-permute-start.25) | collective-permute-done | bytes 491552 | tf_op jit(solution)/shard_map/ppermute | solution.py:25
  142.5 6.1 %multiply_select_fusion.2 = f32[8,8,16,768]{3,2,1,0:T(8,128)S(1)} fusion(f32[8,8,16,768]{3,2,1,0:T(8,128)S(1)} %convolution_add_fusion.2, f32[10,1,16,768]{3,2,1,0:T(8,128)S(1)} %collective-permute-done.25, f32[1,8,16,768]{3,2,1,0:T(8,128)S(1)} %collective-permute-done.23, f32[1,8,16,768]{3,2,1,0:T(8,128)S(1)} %collective-permute-done.22, ...), kind=kOutput, calls=%fused_computation.2 | convolution fusion | flops 73924608 | bytes 14414848 | tf_op jit(solution)/shard_map/kxyz,kv->xyzv/dot_general | solution.py:191
  148.6 11.2 %fusion.71 = f32[14,8,8,16]{3,0,2,1:T(8,128)S(1)} fusion(f32[8,8,16,768]{3,2,1,0:T(8,128)S(1)} %multiply_select_fusion.2, f32[14,768]{1,0:T(8,128)S(1)} %stack.29, f32[768]{0:T(1024)S(1)} %broadcast_multiply_fusion), kind=kOutput, calls=%fused_computation.581 | convolution fusion | flops 132131328 | bytes 3249152 | tf_op jit(solution)/shard_map/kv,xyzv->kxyz/dot_general | solution.py:173
  163.6 11.1 %collective-permute-done.27 = f32[14,8,8,16]{3,2,1,0:T(8,128)S(1)} collective-permute-done((f32[14,8,8,16]{3,2,1,0:T(8,128)S(1)}, f32[14,8,8,16]{3,2,1,0:T(8,128)S(1)}, u32[]{:S(2)}, u32[]{:S(2)}) %collective-permute-start.27) | collective-permute-done | bytes 57376 | tf_op jit(solution)/shard_map/ppermute | solution.py:177
  175.4 3.2 collective-permute-start.28
  183.3 3.1 collective-permute-start.32
  190.7 2.2 collective-permute-done.35
  197.3 2.8 collective-permute-start.36
  209.5 2.7 collective-permute-start.40
  221.3 2.5 collective-permute-start.44
  228.8 22.5 %psum.22 = f32[]{:T(128)} all-reduce(f32[]{:T(128)} %slice_reduce_fusion.1), channel_id=1, replica_groups=mesh['tx'=4,'ty'=2,'vel'=4] {'tx','ty'}, use_global_device_ids=true, to_apply=%region_3.4 | all-reduce | flops 1 | bytes 8 | tf_op jit(solution)/shard_map/psum | solution.py:156
  257.2 2.8 convolution_add_fusion.1
  260.1 4.2 collective-permute-start.49
  264.3 5.5 %collective-permute-done.48 = f32[1,8,16,768]{3,2,1,0:T(8,128)S(1)} collective-permute-done((f32[1,8,16,768]{3,2,1,0:T(8,128)S(1)}, f32[1,8,16,768]{3,2,1,0:T(8,128)S(1)}, u32[]{:S(2)}, u32[]{:S(2)}) %collective-permute-start.48) | collective-permute-done | bytes 393248 | tf_op jit(solution)/shard_map/ppermute | solution.py:23
  269.8 2.8 collective-permute-done.49
  275.7 5.9 %collective-permute-done.50 = f32[10,1,16,768]{3,2,1,0:T(8,128)S(1)} collective-permute-done((f32[10,1,16,768]{3,2,1,0:T(8,128)S(1)}, f32[10,1,16,768]{3,2,1,0:T(8,128)S(1)}, u32[]{:S(2)}, u32[]{:S(2)}) %collective-permute-start.50) | collective-permute-done | bytes 491552 | tf_op jit(solution)/shard_map/ppermute | solution.py:23
  281.5 5.3 %collective-permute-done.51 = f32[10,1,16,768]{3,2,1,0:T(8,128)S(1)} collective-permute-done((f32[10,1,16,768]{3,2,1,0:T(8,128)S(1)}, f32[10,1,16,768]{3,2,1,0:T(8,128)S(1)}, u32[]{:S(2)}, u32[]{:S(2)}) %collective-permute-start.51) | collective-permute-done | bytes 491552 | tf_op jit(solution)/shard_map/ppermute | solution.py:25
  286.9 6.1 %multiply_select_fusion.1 = f32[8,8,16,768]{3,2,1,0:T(8,128)S(1)} fusion(f32[8,8,16,768]{3,2,1,0:T(8,128)S(1)} %convolution_add_fusion.1, f32[10,1,16,768]{3,2,1,0:T(8,128)S(1)} %collective-permute-done.51, f32[1,8,16,768]{3,2,1,0:T(8,128)S(1)} %collective-permute-done.49, f32[1,8,16,768]{3,2,1,0:T(8,128)S(1)} %collective-permute-done.48, ...), kind=kOutput, calls=%fused_computation.1 | convolution fusion | flops 73924608 | bytes 14414848 | tf_op jit(solution)/shard_map/kxyz,kv->xyzv/dot_general | solution.py:191
  293.0 11.2 %fusion.69 = f32[14,8,8,16]{3,0,2,1:T(8,128)S(1)} fusion(f32[8,8,16,768]{3,2,1,0:T(8,128)S(1)} %multiply_select_fusion.1, f32[14,768]{1,0:T(8,128)S(1)} %stack.29, f32[768]{0:T(1024)S(1)} %copy-done.8), kind=kOutput, calls=%fused_computation.579 | convolution fusion | flops 132131328 | bytes 3249152 | tf_op jit(solution)/shard_map/kv,xyzv->kxyz/dot_general | solution.py:173
  308.0 11.1 %collective-permute-done.53 = f32[14,8,8,16]{3,2,1,0:T(8,128)S(1)} collective-permute-done((f32[14,8,8,16]{3,2,1,0:T(8,128)S(1)}, f32[14,8,8,16]{3,2,1,0:T(8,128)S(1)}, u32[]{:S(2)}, u32[]{:S(2)}) %collective-permute-start.53) | collective-permute-done | bytes 57376 | tf_op jit(solution)/shard_map/ppermute | solution.py:177
  319.2 3.8 collective-permute-start.54
  327.8 3.1 collective-permute-start.58
  335.1 2.2 collective-permute-done.61
  341.7 2.8 collective-permute-start.62
  353.9 2.7 collective-permute-start.66
  365.7 2.5 collective-permute-start.70
  373.3 22.8 %psum.23 = f32[]{:T(128)} all-reduce(f32[]{:T(128)} %slice_reduce_fusion), channel_id=1, replica_groups=mesh['tx'=4,'ty'=2,'vel'=4] {'tx','ty'}, use_global_device_ids=true, to_apply=%region_5.6 | all-reduce | flops 1 | bytes 8 | tf_op jit(solution)/shard_map/psum | solution.py:156
  398.9 2.8 convolution_add_fusion
  401.9 3.8 collective-permute-start.75
  405.7 5.9 %collective-permute-done.74 = f32[1,8,16,768]{3,2,1,0:T(8,128)S(1)} collective-permute-done((f32[1,8,16,768]{3,2,1,0:T(8,128)S(1)}, f32[1,8,16,768]{3,2,1,0:T(8,128)S(1)}, u32[]{:S(2)}, u32[]{:S(2)}) %collective-permute-start.74) | collective-permute-done | bytes 393248 | tf_op jit(solution)/shard_map/ppermute | solution.py:23
  411.5 2.4 collective-permute-done.75
  417.0 5.9 %collective-permute-done.76 = f32[10,1,16,768]{3,2,1,0:T(8,128)S(1)} collective-permute-done((f32[10,1,16,768]{3,2,1,0:T(8,128)S(1)}, f32[10,1,16,768]{3,2,1,0:T(8,128)S(1)}, u32[]{:S(2)}, u32[]{:S(2)}) %collective-permute-start.76) | collective-permute-done | bytes 491552 | tf_op jit(solution)/shard_map/ppermute | solution.py:23
  422.9 5.3 %collective-permute-done.77 = f32[10,1,16,768]{3,2,1,0:T(8,128)S(1)} collective-permute-done((f32[10,1,16,768]{3,2,1,0:T(8,128)S(1)}, f32[10,1,16,768]{3,2,1,0:T(8,128)S(1)}, u32[]{:S(2)}, u32[]{:S(2)}) %collective-permute-start.77) | collective-permute-done | bytes 491552 | tf_op jit(solution)/shard_map/ppermute | solution.py:25
  428.2 7.9 %multiply_select_fusion = f32[8,8,16,768]{3,2,1,0:T(8,128)} fusion(f32[8,8,16,768]{3,2,1,0:T(8,128)S(1)} %convolution_add_fusion, f32[10,1,16,768]{3,2,1,0:T(8,128)S(1)} %collective-permute-done.77, f32[1,8,16,768]{3,2,1,0:T(8,128)S(1)} %collective-permute-done.75, f32[1,8,16,768]{3,2,1,0:T(8,128)S(1)} %collective-permute-done.74, ...), kind=kOutput, calls=%fused_computation | convolution fusion | flops 73924608 | bytes 14414848 | tf_op jit(solution)/shard_map/kxyz,kv->xyzv/dot_general | solution.py:191
  (422 shorter events, 147.3 us)
Async XLA Ops:
  19.7 13.7 %collective-permute-start.1 = (f32[14,8,8,16]{3,2,1,0:T(8,128)S(1)}, f32[14,8,8,16]{3,2,1,0:T(8,128)S(1)}, u32[]{:S(2)}, u32[]{:S(2)}) collective-permute-start(f32[14,8,8,16]{3,2,1,0:T(8,128)S(1)} %copy_add_fusion.2), channel_id=1, source_target_pairs={{0,2},{1,3},{2,0},{3,1},{4,6},{5,7},{6,4},{7,5},{8,10},{9,11},{10,... | collective-permute-start | bytes 172040 | tf_op jit(solution)/shard_map/ppermute | solution.py:177
  33.5 5.8 %collective-permute-start.3 = (f32[5,1,8,16]{3,2,1,0:T(8,128)S(1)}, f32[5,1,8,16]{3,2,1,0:T(8,128)S(1)}, u32[]{:S(2)}, u32[]{:S(2)}) collective-permute-start(f32[5,1,8,16]{3,2,1,0:T(8,128)S(1)} %get-tuple-element.84), channel_id=1, source_target_pairs={{0,8},{8,16},{16,24},{24,0},{1,9},{9,17},{17,25},{25,1},{2,10},{10... | collective-permute-start | bytes 7688 | tf_op jit(solution)/shard_map/ppermute | solution.py:23
  39.4 6.1 %collective-permute-start.5 = (f32[5,10,1,16]{3,2,1,0:T(1,128)S(1)}, f32[5,10,1,16]{3,2,1,0:T(1,128)S(1)}, u32[]{:S(2)}, u32[]{:S(2)}) collective-permute-start(f32[5,10,1,16]{3,2,1,0:T(1,128)S(1)} %get-tuple-element.162), channel_id=1, source_target_pairs={{0,4},{4,0},{1,5},{5,1},{2,6},{6,2},{3,7},{7,3},{8,12},{12,8},{9,1... | collective-permute-start | bytes 9608 | tf_op jit(solution)/shard_map/ppermute | solution.py:23
  41.5 6.1 %collective-permute-start.7 = (f32[13,1,8,16]{3,2,1,0:T(8,128)S(1)}, f32[13,1,8,16]{3,2,1,0:T(8,128)S(1)}, u32[]{:S(2)}, u32[]{:S(2)}) collective-permute-start(f32[13,1,8,16]{3,2,1,0:T(8,128)S(1)} %get-tuple-element.90), channel_id=1, source_target_pairs={{0,8},{8,16},{16,24},{24,0},{1,9},{9,17},{17,25},{25,1},{2,10},{10... | collective-permute-start | bytes 19976 | tf_op jit(solution)/shard_map/ppermute | solution.py:23
  42.9 4.9 %collective-permute-start.6 = (f32[13,1,8,16]{3,2,1,0:T(8,128)S(1)}, f32[13,1,8,16]{3,2,1,0:T(8,128)S(1)}, u32[]{:S(2)}, u32[]{:S(2)}) collective-permute-start(f32[13,1,8,16]{3,2,1,0:T(8,128)S(1)} %get-tuple-element.91), channel_id=1, source_target_pairs={{8,0},{16,8},{24,16},{0,24},{9,1},{17,9},{25,17},{1,25},{10,2},{18... | collective-permute-start | bytes 19976 | tf_op jit(solution)/shard_map/ppermute | solution.py:25
  56.1 5.6 %collective-permute-start.11 = (f32[5,1,8,16]{3,2,1,0:T(8,128)S(1)}, f32[5,1,8,16]{3,2,1,0:T(8,128)S(1)}, u32[]{:S(2)}, u32[]{:S(2)}) collective-permute-start(f32[5,1,8,16]{3,2,1,0:T(8,128)S(1)} %get-tuple-element.184), channel_id=1, source_target_pairs={{0,8},{8,16},{16,24},{24,0},{1,9},{9,17},{17,25},{25,1},{2,10},{10... | collective-permute-start | bytes 7688 | tf_op jit(solution)/shard_map/ppermute | solution.py:23
  67.6 5.7 %collective-permute-start.15 = (f32[5,1,8,16]{3,2,1,0:T(8,128)S(1)}, f32[5,1,8,16]{3,2,1,0:T(8,128)S(1)}, u32[]{:S(2)}, u32[]{:S(2)}) collective-permute-start(f32[5,1,8,16]{3,2,1,0:T(8,128)S(1)} %get-tuple-element.182), channel_id=1, source_target_pairs={{0,8},{8,16},{16,24},{24,0},{1,9},{9,17},{17,25},{25,1},{2,10},{10... | collective-permute-start | bytes 7688 | tf_op jit(solution)/shard_map/ppermute | solution.py:23
  79.6 5.7 %collective-permute-start.19 = (f32[5,1,8,16]{3,2,1,0:T(8,128)S(1)}, f32[5,1,8,16]{3,2,1,0:T(8,128)S(1)}, u32[]{:S(2)}, u32[]{:S(2)}) collective-permute-start(f32[5,1,8,16]{3,2,1,0:T(8,128)S(1)} %get-tuple-element.180), channel_id=1, source_target_pairs={{0,8},{8,16},{16,24},{24,0},{1,9},{9,17},{17,25},{25,1},{2,10},{10... | collective-permute-start | bytes 7688 | tf_op jit(solution)/shard_map/ppermute | solution.py:23
  85.4 25.4 %collective-permute-start.21 = (f32[5,10,1,16]{3,2,1,0:T(1,128)S(1)}, f32[5,10,1,16]{3,2,1,0:T(1,128)S(1)}, u32[]{:S(2)}, u32[]{:S(2)}) collective-permute-start(f32[5,10,1,16]{3,2,1,0:T(1,128)S(1)} %get-tuple-element.150), channel_id=1, source_target_pairs={{0,4},{4,0},{1,5},{5,1},{2,6},{6,2},{3,7},{7,3},{8,12},{12,8},{9,1... | collective-permute-start | bytes 9608 | tf_op jit(solution)/shard_map/ppermute | solution.py:23
  86.2 24.6 %collective-permute-start.20 = (f32[5,10,1,16]{3,2,1,0:T(1,128)S(1)}, f32[5,10,1,16]{3,2,1,0:T(1,128)S(1)}, u32[]{:S(2)}, u32[]{:S(2)}) collective-permute-start(f32[5,10,1,16]{3,2,1,0:T(1,128)S(1)} %get-tuple-element.151), channel_id=1, source_target_pairs={{4,0},{0,4},{5,1},{1,5},{6,2},{2,6},{7,3},{3,7},{12,8},{8,12},{13,... | collective-permute-start | bytes 9608 | tf_op jit(solution)/shard_map/ppermute | solution.py:25
  115.7 9.7 %collective-permute-start.22 = (f32[1,8,16,768]{3,2,1,0:T(8,128)S(1)}, f32[1,8,16,768]{3,2,1,0:T(8,128)S(1)}, u32[]{:S(2)}, u32[]{:S(2)}) collective-permute-start(f32[1,8,16,768]{3,2,1,0:T(8,128)S(1)} %get-tuple-element.60), channel_id=1, source_target_pairs={{0,8},{8,16},{16,24},{24,0},{1,9},{9,17},{17,25},{25,1},{2,10},{10... | collective-permute-start | bytes 1179656 | tf_op jit(solution)/shard_map/ppermute | solution.py:23
  115.7 12.4 %collective-permute-start.23 = (f32[1,8,16,768]{3,2,1,0:T(8,128)S(1)}, f32[1,8,16,768]{3,2,1,0:T(8,128)S(1)}, u32[]{:S(2)}, u32[]{:S(2)}) collective-permute-start(f32[1,8,16,768]{3,2,1,0:T(8,128)S(1)} %get-tuple-element.61), channel_id=1, source_target_pairs={{8,0},{16,8},{24,16},{0,24},{9,1},{17,9},{25,17},{1,25},{10,2},{18... | collective-permute-start | bytes 1179656 | tf_op jit(solution)/shard_map/ppermute | solution.py:25
  128.3 8.9 %collective-permute-start.24 = (f32[10,1,16,768]{3,2,1,0:T(8,128)S(1)}, f32[10,1,16,768]{3,2,1,0:T(8,128)S(1)}, u32[]{:S(2)}, u32[]{:S(2)}) collective-permute-start(f32[10,1,16,768]{3,2,1,0:T(8,128)S(1)} %get-tuple-element.42), channel_id=1, source_target_pairs={{0,4},{4,0},{1,5},{5,1},{2,6},{6,2},{3,7},{7,3},{8,12},{12,8},{9,1... | collective-permute-start | bytes 1474568 | tf_op jit(solution)/shard_map/ppermute | solution.py:23
  128.3 14.1 %collective-permute-start.25 = (f32[10,1,16,768]{3,2,1,0:T(8,128)S(1)}, f32[10,1,16,768]{3,2,1,0:T(8,128)S(1)}, u32[]{:S(2)}, u32[]{:S(2)}) collective-permute-start(f32[10,1,16,768]{3,2,1,0:T(8,128)S(1)} %get-tuple-element.43), channel_id=1, source_target_pairs={{4,0},{0,4},{5,1},{1,5},{6,2},{2,6},{7,3},{3,7},{12,8},{8,12},{13,... | collective-permute-start | bytes 1474568 | tf_op jit(solution)/shard_map/ppermute | solution.py:25
  162.0 12.6 %collective-permute-start.27 = (f32[14,8,8,16]{3,2,1,0:T(8,128)S(1)}, f32[14,8,8,16]{3,2,1,0:T(8,128)S(1)}, u32[]{:S(2)}, u32[]{:S(2)}) collective-permute-start(f32[14,8,8,16]{3,2,1,0:T(8,128)S(1)} %copy_add_fusion.1), channel_id=1, source_target_pairs={{0,2},{1,3},{2,0},{3,1},{4,6},{5,7},{6,4},{7,5},{8,10},{9,11},{10,... | collective-permute-start | bytes 172040 | tf_op jit(solution)/shard_map/ppermute | solution.py:177
  174.7 5.6 %collective-permute-start.29 = (f32[5,1,8,16]{3,2,1,0:T(8,128)S(1)}, f32[5,1,8,16]{3,2,1,0:T(8,128)S(1)}, u32[]{:S(2)}, u32[]{:S(2)}) collective-permute-start(f32[5,1,8,16]{3,2,1,0:T(8,128)S(1)} %get-tuple-element.82), channel_id=1, source_target_pairs={{0,8},{8,16},{16,24},{24,0},{1,9},{9,17},{17,25},{25,1},{2,10},{10... | collective-permute-start | bytes 7688 | tf_op jit(solution)/shard_map/ppermute | solution.py:23
  175.4 4.9 %collective-permute-start.28 = (f32[5,1,8,16]{3,2,1,0:T(8,128)S(1)}, f32[5,1,8,16]{3,2,1,0:T(8,128)S(1)}, u32[]{:S(2)}, u32[]{:S(2)}) collective-permute-start(f32[5,1,8,16]{3,2,1,0:T(8,128)S(1)} %get-tuple-element.83), channel_id=1, source_target_pairs={{8,0},{16,8},{24,16},{0,24},{9,1},{17,9},{25,17},{1,25},{10,2},{18... | collective-permute-start | bytes 7688 | tf_op jit(solution)/shard_map/ppermute | solution.py:25
  180.4 6.0 %collective-permute-start.31 = (f32[5,10,1,16]{3,2,1,0:T(1,128)S(1)}, f32[5,10,1,16]{3,2,1,0:T(1,128)S(1)}, u32[]{:S(2)}, u32[]{:S(2)}) collective-permute-start(f32[5,10,1,16]{3,2,1,0:T(1,128)S(1)} %get-tuple-element.146), channel_id=1, source_target_pairs={{0,4},{4,0},{1,5},{5,1},{2,6},{6,2},{3,7},{7,3},{8,12},{12,8},{9,1... | collective-permute-start | bytes 9608 | tf_op jit(solution)/shard_map/ppermute | solution.py:23
  180.5 6.0 %collective-permute-start.30 = (f32[5,10,1,16]{3,2,1,0:T(1,128)S(1)}, f32[5,10,1,16]{3,2,1,0:T(1,128)S(1)}, u32[]{:S(2)}, u32[]{:S(2)}) collective-permute-start(f32[5,10,1,16]{3,2,1,0:T(1,128)S(1)} %get-tuple-element.147), channel_id=1, source_target_pairs={{4,0},{0,4},{5,1},{1,5},{6,2},{2,6},{7,3},{3,7},{12,8},{8,12},{13,... | collective-permute-start | bytes 9608 | tf_op jit(solution)/shard_map/ppermute | solution.py:25
  182.5 6.0 %collective-permute-start.33 = (f32[13,1,8,16]{3,2,1,0:T(8,128)S(1)}, f32[13,1,8,16]{3,2,1,0:T(8,128)S(1)}, u32[]{:S(2)}, u32[]{:S(2)}) collective-permute-start(f32[13,1,8,16]{3,2,1,0:T(8,128)S(1)} %get-tuple-element.88), channel_id=1, source_target_pairs={{0,8},{8,16},{16,24},{24,0},{1,9},{9,17},{17,25},{25,1},{2,10},{10... | collective-permute-start | bytes 19976 | tf_op jit(solution)/shard_map/ppermute | solution.py:23
  183.3 5.2 %collective-permute-start.32 = (f32[13,1,8,16]{3,2,1,0:T(8,128)S(1)}, f32[13,1,8,16]{3,2,1,0:T(8,128)S(1)}, u32[]{:S(2)}, u32[]{:S(2)}) collective-permute-start(f32[13,1,8,16]{3,2,1,0:T(8,128)S(1)} %get-tuple-element.89), channel_id=1, source_target_pairs={{8,0},{16,8},{24,16},{0,24},{9,1},{17,9},{25,17},{1,25},{10,2},{18... | collective-permute-start | bytes 19976 | tf_op jit(solution)/shard_map/ppermute | solution.py:25
  188.8 4.9 %collective-permute-start.34 = (f32[13,10,1,16]{3,2,1,0:T(1,128)S(1)}, f32[13,10,1,16]{3,2,1,0:T(1,128)S(1)}, u32[]{:S(2)}, u32[]{:S(2)}) collective-permute-start(f32[13,10,1,16]{3,2,1,0:T(1,128)S(1)} %get-tuple-element.75), channel_id=1, source_target_pairs={{4,0},{0,4},{5,1},{1,5},{6,2},{2,6},{7,3},{3,7},{12,8},{8,12},{13,... | collective-permute-start | bytes 24968 | tf_op jit(solution)/shard_map/ppermute | solution.py:25
  196.1 5.7 %collective-permute-start.37 = (f32[5,1,8,16]{3,2,1,0:T(8,128)S(1)}, f32[5,1,8,16]{3,2,1,0:T(8,128)S(1)}, u32[]{:S(2)}, u32[]{:S(2)}) collective-permute-start(f32[5,1,8,16]{3,2,1,0:T(8,128)S(1)} %get-tuple-element.176), channel_id=1, source_target_pairs={{0,8},{8,16},{16,24},{24,0},{1,9},{9,17},{17,25},{25,1},{2,10},{10... | collective-permute-start | bytes 7688 | tf_op jit(solution)/shard_map/ppermute | solution.py:23
  208.2 5.7 %collective-permute-start.41 = (f32[5,1,8,16]{3,2,1,0:T(8,128)S(1)}, f32[5,1,8,16]{3,2,1,0:T(8,128)S(1)}, u32[]{:S(2)}, u32[]{:S(2)}) collective-permute-start(f32[5,1,8,16]{3,2,1,0:T(8,128)S(1)} %get-tuple-element.174), channel_id=1, source_target_pairs={{0,8},{8,16},{16,24},{24,0},{1,9},{9,17},{17,25},{25,1},{2,10},{10... | collective-permute-start | bytes 7688 | tf_op jit(solution)/shard_map/ppermute | solution.py:23
  219.7 5.8 %collective-permute-start.45 = (f32[5,1,8,16]{3,2,1,0:T(8,128)S(1)}, f32[5,1,8,16]{3,2,1,0:T(8,128)S(1)}, u32[]{:S(2)}, u32[]{:S(2)}) collective-permute-start(f32[5,1,8,16]{3,2,1,0:T(8,128)S(1)} %get-tuple-element.172), channel_id=1, source_target_pairs={{0,8},{8,16},{16,24},{24,0},{1,9},{9,17},{17,25},{25,1},{2,10},{10... | collective-permute-start | bytes 7688 | tf_op jit(solution)/shard_map/ppermute | solution.py:23
  226.2 25.7 %collective-permute-start.47 = (f32[5,10,1,16]{3,2,1,0:T(1,128)}, f32[5,10,1,16]{3,2,1,0:T(1,128)}, u32[]{:S(2)}, u32[]{:S(2)}) collective-permute-start(f32[5,10,1,16]{3,2,1,0:T(1,128)} %get-tuple-element.134), channel_id=1, source_target_pairs={{0,4},{4,0},{1,5},{5,1},{2,6},{6,2},{3,7},{7,3},{8,12},{12,8},{9,1... | collective-permute-start | bytes 9608 | tf_op jit(solution)/shard_map/ppermute | solution.py:23
  227.4 24.5 %collective-permute-start.46 = (f32[5,10,1,16]{3,2,1,0:T(1,128)}, f32[5,10,1,16]{3,2,1,0:T(1,128)}, u32[]{:S(2)}, u32[]{:S(2)}) collective-permute-start(f32[5,10,1,16]{3,2,1,0:T(1,128)} %get-tuple-element.135), channel_id=1, source_target_pairs={{4,0},{0,4},{5,1},{1,5},{6,2},{2,6},{7,3},{3,7},{12,8},{8,12},{13,... | collective-permute-start | bytes 9608 | tf_op jit(solution)/shard_map/ppermute | solution.py:25
  260.0 9.7 %collective-permute-start.48 = (f32[1,8,16,768]{3,2,1,0:T(8,128)S(1)}, f32[1,8,16,768]{3,2,1,0:T(8,128)S(1)}, u32[]{:S(2)}, u32[]{:S(2)}) collective-permute-start(f32[1,8,16,768]{3,2,1,0:T(8,128)S(1)} %get-tuple-element.54), channel_id=1, source_target_pairs={{0,8},{8,16},{16,24},{24,0},{1,9},{9,17},{17,25},{25,1},{2,10},{10... | collective-permute-start | bytes 1179656 | tf_op jit(solution)/shard_map/ppermute | solution.py:23
  260.1 12.4 %collective-permute-start.49 = (f32[1,8,16,768]{3,2,1,0:T(8,128)S(1)}, f32[1,8,16,768]{3,2,1,0:T(8,128)S(1)}, u32[]{:S(2)}, u32[]{:S(2)}) collective-permute-start(f32[1,8,16,768]{3,2,1,0:T(8,128)S(1)} %get-tuple-element.55), channel_id=1, source_target_pairs={{8,0},{16,8},{24,16},{0,24},{9,1},{17,9},{25,17},{1,25},{10,2},{18... | collective-permute-start | bytes 1179656 | tf_op jit(solution)/shard_map/ppermute | solution.py:25
  272.6 8.9 %collective-permute-start.50 = (f32[10,1,16,768]{3,2,1,0:T(8,128)S(1)}, f32[10,1,16,768]{3,2,1,0:T(8,128)S(1)}, u32[]{:S(2)}, u32[]{:S(2)}) collective-permute-start(f32[10,1,16,768]{3,2,1,0:T(8,128)S(1)} %get-tuple-element.40), channel_id=1, source_target_pairs={{0,4},{4,0},{1,5},{5,1},{2,6},{6,2},{3,7},{7,3},{8,12},{12,8},{9,1... | collective-permute-start | bytes 1474568 | tf_op jit(solution)/shard_map/ppermute | solution.py:23
  272.7 14.1 %collective-permute-start.51 = (f32[10,1,16,768]{3,2,1,0:T(8,128)S(1)}, f32[10,1,16,768]{3,2,1,0:T(8,128)S(1)}, u32[]{:S(2)}, u32[]{:S(2)}) collective-permute-start(f32[10,1,16,768]{3,2,1,0:T(8,128)S(1)} %get-tuple-element.41), channel_id=1, source_target_pairs={{4,0},{0,4},{5,1},{1,5},{6,2},{2,6},{7,3},{3,7},{12,8},{8,12},{13,... | collective-permute-start | bytes 1474568 | tf_op jit(solution)/shard_map/ppermute | solution.py:25
  306.4 12.6 %collective-permute-start.53 = (f32[14,8,8,16]{3,2,1,0:T(8,128)S(1)}, f32[14,8,8,16]{3,2,1,0:T(8,128)S(1)}, u32[]{:S(2)}, u32[]{:S(2)}) collective-permute-start(f32[14,8,8,16]{3,2,1,0:T(8,128)S(1)} %copy_add_fusion), channel_id=1, source_target_pairs={{0,2},{1,3},{2,0},{3,1},{4,6},{5,7},{6,4},{7,5},{8,10},{9,11},{10,... | collective-permute-start | bytes 172040 | tf_op jit(solution)/shard_map/ppermute | solution.py:177
  319.1 5.6 %collective-permute-start.55 = (f32[5,1,8,16]{3,2,1,0:T(8,128)S(1)}, f32[5,1,8,16]{3,2,1,0:T(8,128)S(1)}, u32[]{:S(2)}, u32[]{:S(2)}) collective-permute-start(f32[5,1,8,16]{3,2,1,0:T(8,128)S(1)} %get-tuple-element.80), channel_id=1, source_target_pairs={{0,8},{8,16},{16,24},{24,0},{1,9},{9,17},{17,25},{25,1},{2,10},{10... | collective-permute-start | bytes 7688 | tf_op jit(solution)/shard_map/ppermute | solution.py:23
  319.2 5.6 %collective-permute-start.54 = (f32[5,1,8,16]{3,2,1,0:T(8,128)S(1)}, f32[5,1,8,16]{3,2,1,0:T(8,128)S(1)}, u32[]{:S(2)}, u32[]{:S(2)}) collective-permute-start(f32[5,1,8,16]{3,2,1,0:T(8,128)S(1)} %get-tuple-element.81), channel_id=1, source_target_pairs={{8,0},{16,8},{24,16},{0,24},{9,1},{17,9},{25,17},{1,25},{10,2},{18... | collective-permute-start | bytes 7688 | tf_op jit(solution)/shard_map/ppermute | solution.py:25
  324.8 6.0 %collective-permute-start.57 = (f32[5,10,1,16]{3,2,1,0:T(1,128)S(1)}, f32[5,10,1,16]{3,2,1,0:T(1,128)S(1)}, u32[]{:S(2)}, u32[]{:S(2)}) collective-permute-start(f32[5,10,1,16]{3,2,1,0:T(1,128)S(1)} %get-tuple-element.130), channel_id=1, source_target_pairs={{0,4},{4,0},{1,5},{5,1},{2,6},{6,2},{3,7},{7,3},{8,12},{12,8},{9,1... | collective-permute-start | bytes 9608 | tf_op jit(solution)/shard_map/ppermute | solution.py:23
  324.9 6.0 %collective-permute-start.56 = (f32[5,10,1,16]{3,2,1,0:T(1,128)S(1)}, f32[5,10,1,16]{3,2,1,0:T(1,128)S(1)}, u32[]{:S(2)}, u32[]{:S(2)}) collective-permute-start(f32[5,10,1,16]{3,2,1,0:T(1,128)S(1)} %get-tuple-element.131), channel_id=1, source_target_pairs={{4,0},{0,4},{5,1},{1,5},{6,2},{2,6},{7,3},{3,7},{12,8},{8,12},{13,... | collective-permute-start | bytes 9608 | tf_op jit(solution)/shard_map/ppermute | solution.py:25
  326.9 6.0 %collective-permute-start.59 = (f32[13,1,8,16]{3,2,1,0:T(8,128)S(1)}, f32[13,1,8,16]{3,2,1,0:T(8,128)S(1)}, u32[]{:S(2)}, u32[]{:S(2)}) collective-permute-start(f32[13,1,8,16]{3,2,1,0:T(8,128)S(1)} %get-tuple-element.86), channel_id=1, source_target_pairs={{0,8},{8,16},{16,24},{24,0},{1,9},{9,17},{17,25},{25,1},{2,10},{10... | collective-permute-start | bytes 19976 | tf_op jit(solution)/shard_map/ppermute | solution.py:23
  327.8 5.2 %collective-permute-start.58 = (f32[13,1,8,16]{3,2,1,0:T(8,128)S(1)}, f32[13,1,8,16]{3,2,1,0:T(8,128)S(1)}, u32[]{:S(2)}, u32[]{:S(2)}) collective-permute-start(f32[13,1,8,16]{3,2,1,0:T(8,128)S(1)} %get-tuple-element.87), channel_id=1, source_target_pairs={{8,0},{16,8},{24,16},{0,24},{9,1},{17,9},{25,17},{1,25},{10,2},{18... | collective-permute-start | bytes 19976 | tf_op jit(solution)/shard_map/ppermute | solution.py:25
  333.2 4.9 %collective-permute-start.60 = (f32[13,10,1,16]{3,2,1,0:T(1,128)S(1)}, f32[13,10,1,16]{3,2,1,0:T(1,128)S(1)}, u32[]{:S(2)}, u32[]{:S(2)}) collective-permute-start(f32[13,10,1,16]{3,2,1,0:T(1,128)S(1)} %get-tuple-element.71), channel_id=1, source_target_pairs={{4,0},{0,4},{5,1},{1,5},{6,2},{2,6},{7,3},{3,7},{12,8},{8,12},{13,... | collective-permute-start | bytes 24968 | tf_op jit(solution)/shard_map/ppermute | solution.py:25
  340.5 5.7 %collective-permute-start.63 = (f32[5,1,8,16]{3,2,1,0:T(8,128)S(1)}, f32[5,1,8,16]{3,2,1,0:T(8,128)S(1)}, u32[]{:S(2)}, u32[]{:S(2)}) collective-permute-start(f32[5,1,8,16]{3,2,1,0:T(8,128)S(1)} %get-tuple-element.168), channel_id=1, source_target_pairs={{0,8},{8,16},{16,24},{24,0},{1,9},{9,17},{17,25},{25,1},{2,10},{10... | collective-permute-start | bytes 7688 | tf_op jit(solution)/shard_map/ppermute | solution.py:23
  352.6 5.7 %collective-permute-start.67 = (f32[5,1,8,16]{3,2,1,0:T(8,128)S(1)}, f32[5,1,8,16]{3,2,1,0:T(8,128)S(1)}, u32[]{:S(2)}, u32[]{:S(2)}) collective-permute-start(f32[5,1,8,16]{3,2,1,0:T(8,128)S(1)} %get-tuple-element.166), channel_id=1, source_target_pairs={{0,8},{8,16},{16,24},{24,0},{1,9},{9,17},{17,25},{25,1},{2,10},{10... | collective-permute-start | bytes 7688 | tf_op jit(solution)/shard_map/ppermute | solution.py:23
  364.1 5.8 %collective-permute-start.71 = (f32[5,1,8,16]{3,2,1,0:T(8,128)S(1)}, f32[5,1,8,16]{3,2,1,0:T(8,128)S(1)}, u32[]{:S(2)}, u32[]{:S(2)}) collective-permute-start(f32[5,1,8,16]{3,2,1,0:T(8,128)S(1)} %get-tuple-element.164), channel_id=1, source_target_pairs={{0,8},{8,16},{16,24},{24,0},{1,9},{9,17},{17,25},{25,1},{2,10},{10... | collective-permute-start | bytes 7688 | tf_op jit(solution)/shard_map/ppermute | solution.py:23
  370.6 26.2 %collective-permute-start.73 = (f32[5,10,1,16]{3,2,1,0:T(1,128)}, f32[5,10,1,16]{3,2,1,0:T(1,128)S(1)}, u32[]{:S(2)}, u32[]{:S(2)}) collective-permute-start(f32[5,10,1,16]{3,2,1,0:T(1,128)} %get-tuple-element.118), channel_id=1, source_target_pairs={{0,4},{4,0},{1,5},{5,1},{2,6},{6,2},{3,7},{7,3},{8,12},{12,8},{9,1... | collective-permute-start | bytes 9608 | tf_op jit(solution)/shard_map/ppermute | solution.py:23
  371.8 25.0 %collective-permute-start.72 = (f32[5,10,1,16]{3,2,1,0:T(1,128)}, f32[5,10,1,16]{3,2,1,0:T(1,128)S(1)}, u32[]{:S(2)}, u32[]{:S(2)}) collective-permute-start(f32[5,10,1,16]{3,2,1,0:T(1,128)} %get-tuple-element.119), channel_id=1, source_target_pairs={{4,0},{0,4},{5,1},{1,5},{6,2},{2,6},{7,3},{3,7},{12,8},{8,12},{13,... | collective-permute-start | bytes 9608 | tf_op jit(solution)/shard_map/ppermute | solution.py:25
  401.8 9.7 %collective-permute-start.74 = (f32[1,8,16,768]{3,2,1,0:T(8,128)S(1)}, f32[1,8,16,768]{3,2,1,0:T(8,128)S(1)}, u32[]{:S(2)}, u32[]{:S(2)}) collective-permute-start(f32[1,8,16,768]{3,2,1,0:T(8,128)S(1)} %get-tuple-element.48), channel_id=1, source_target_pairs={{0,8},{8,16},{16,24},{24,0},{1,9},{9,17},{17,25},{25,1},{2,10},{10... | collective-permute-start | bytes 1179656 | tf_op jit(solution)/shard_map/ppermute | solution.py:23
  401.9 12.0 %collective-permute-start.75 = (f32[1,8,16,768]{3,2,1,0:T(8,128)S(1)}, f32[1,8,16,768]{3,2,1,0:T(8,128)S(1)}, u32[]{:S(2)}, u32[]{:S(2)}) collective-permute-start(f32[1,8,16,768]{3,2,1,0:T(8,128)S(1)} %get-tuple-element.49), channel_id=1, source_target_pairs={{8,0},{16,8},{24,16},{0,24},{9,1},{17,9},{25,17},{1,25},{10,2},{18... | collective-permute-start | bytes 1179656 | tf_op jit(solution)/shard_map/ppermute | solution.py:25
  414.0 8.9 %collective-permute-start.76 = (f32[10,1,16,768]{3,2,1,0:T(8,128)S(1)}, f32[10,1,16,768]{3,2,1,0:T(8,128)S(1)}, u32[]{:S(2)}, u32[]{:S(2)}) collective-permute-start(f32[10,1,16,768]{3,2,1,0:T(8,128)S(1)} %get-tuple-element.38), channel_id=1, source_target_pairs={{0,4},{4,0},{1,5},{5,1},{2,6},{6,2},{3,7},{7,3},{8,12},{12,8},{9,1... | collective-permute-start | bytes 1474568 | tf_op jit(solution)/shard_map/ppermute | solution.py:23
  414.1 14.1 %collective-permute-start.77 = (f32[10,1,16,768]{3,2,1,0:T(8,128)S(1)}, f32[10,1,16,768]{3,2,1,0:T(8,128)S(1)}, u32[]{:S(2)}, u32[]{:S(2)}) collective-permute-start(f32[10,1,16,768]{3,2,1,0:T(8,128)S(1)} %get-tuple-element.39), channel_id=1, source_target_pairs={{4,0},{0,4},{5,1},{1,5},{6,2},{2,6},{7,3},{3,7},{12,8},{8,12},{13,... | collective-permute-start | bytes 1474568 | tf_op jit(solution)/shard_map/ppermute | solution.py:25
  (67 other events, 1016.8 us)
